TPU v7x, 32 devices: a whole 2x2x4 slice. The times are simulated.
32 devices in a mesh: ctx: 8 (over z, y), tp: 4 (over x, core).
Axes of the slice: x: 2, y: 2, z: 4, core: 2. Of those that a mesh axis runs over, the one named last changes fastest.
Arguments:
- block_input: bfloat16 [2048, 2048], P(('ctx', 'tp')), may hold values from -6 to 6
- qkv_weight: bfloat16 [3, 2048, 2048], P(None, 'ctx', 'tp'), may hold values from -1 to 1
- out_weight: bfloat16 [2048, 2048], P('tp', 'ctx'), may hold values from -4 to 4
- gate_up_weight: bfloat16 [2, 2048, 8192], P(None, 'ctx', 'tp'), may hold values from -0.125 to 0.125
- down_weight: bfloat16 [8192, 2048], P('tp', 'ctx'), may hold values from -0.0625 to 0.0625
- norm_gains: bfloat16 [2, 2048], P(None, 'ctx'), may hold values from 0.5 to 1.5
- positions: int32 [2048], replicated, may hold values from 0 to 2047, as said below
- layer_output_gradient: bfloat16 [2048, 2048], P(('ctx', 'tp')), may hold values from -6 to 6
Outputs:
- block_output: bfloat16 [2048, 2048], P(('ctx', 'tp'))
- layer_input_gradient: float32 [2048, 2048], P(('ctx', 'tp'))
- qkv_grad: float32 [3, 2048, 2048], P(None, 'ctx', 'tp')
- out_weight_grad: float32 [2048, 2048], P('tp', 'ctx')
- gate_up_grad: float32 [2, 2048, 8192], P(None, 'ctx', 'tp')
- down_grad: float32 [8192, 2048], P('tp', 'ctx')
- gain_grad: float32 [2, 2048], P(None, ('ctx', 'tp'))
Inputs may be any that keep to these rules, and one draw needn't show every extreme that they name: Each value appears once; the rows of one ctx index hold two runs of 128 consecutive positions, runs number b and 15 - b, with b differing between indices.
All inputs are finite; a program needn't handle non-finite values.
Results may differ from a plain program's by a relative error of at most 0.019.
Values may be sent and summed in bfloat16 or wider, within the bound.
A program may use at most 256 MiB of HBM per device.

v0:
```python
import math

import jax
import jax.numpy as jnp
from jax import lax
from jax.sharding import PartitionSpec as P

HD = 64


norm_eps = 1e-05
rope_base = 130000.0


def inv_rms(values):
    return lax.rsqrt(jnp.mean(values * values, axis=-1, keepdims=True) + norm_eps)


def rope_tables(where_at, head_dim):
    half_dim = head_dim // 2
    inv_freq = rope_base ** (-(jnp.arange(half_dim, dtype=jnp.float32) * 2.0 / head_dim))
    angles = where_at.astype(jnp.float32)[:, None] * inv_freq[None, :]
    return (jnp.cos(angles)[:, None, :], jnp.sin(angles)[:, None, :])


def rotate(values, cos_tab, sin_tab, n_heads, head_dim):
    shaped = values.reshape(values.shape[0], n_heads, head_dim)
    half_dim = head_dim // 2
    lower_half, upper_half = (shaped[..., :half_dim], shaped[..., half_dim:])
    turned = jnp.concatenate(
        [lower_half * cos_tab - upper_half * sin_tab, upper_half * cos_tab + lower_half * sin_tab],
        axis=-1,
    )
    return turned.reshape(values.shape[0], n_heads * head_dim)


def unrotate(values, cos_tab, sin_tab, n_heads, head_dim):
    shaped = values.reshape(values.shape[0], n_heads, head_dim)
    half_dim = head_dim // 2
    lower_half, upper_half = (shaped[..., :half_dim], shaped[..., half_dim:])
    turned = jnp.concatenate(
        [lower_half * cos_tab + upper_half * sin_tab, upper_half * cos_tab - lower_half * sin_tab],
        axis=-1,
    )
    return turned.reshape(values.shape[0], n_heads * head_dim)


def masked_scores(query_blk, key_blk, query_pos, key_pos, score_scale):
    scores = (
        jnp.einsum("qhd,khd->hqk", query_blk, key_blk, preferred_element_type=jnp.float32)
        * score_scale
    )
    visible = key_pos[None, None, :] <= query_pos[None, :, None]
    return (jnp.where(visible, scores, -1e30), visible)


def block_grads(
    query_blk, grad_blk, lse_rows, delta_rows, query_pos, key_blk, value_blk, key_pos, score_scale
):
    scores, visible = masked_scores(query_blk, key_blk, query_pos, key_pos, score_scale)
    prob_rows = jnp.where(visible, jnp.exp(scores - lse_rows[..., None]), 0.0)
    probs_bf = prob_rows.astype(jnp.bfloat16)
    prob_grad = jnp.einsum("qhd,khd->hqk", grad_blk, value_blk, preferred_element_type=jnp.float32)
    score_grad = (prob_rows * (prob_grad - delta_rows[..., None]) * score_scale).astype(
        jnp.bfloat16
    )
    query_part = jnp.einsum("hqk,khd->qhd", score_grad, key_blk, preferred_element_type=jnp.float32)
    key_part = jnp.einsum("hqk,qhd->khd", score_grad, query_blk, preferred_element_type=jnp.float32)
    value_part = jnp.einsum("hqk,qhd->khd", probs_bf, grad_blk, preferred_element_type=jnp.float32)
    return (query_part, key_part, value_part)


def body(
    block_input,
    qkv_weight,
    out_weight,
    gate_up_weight,
    down_weight,
    norm_gains,
    positions,
    layer_output_gradient,
):
    qkv_full, out_full, gate_up_full, down_full, gains_full = (
        lax.all_gather(qkv_weight, "ctx", axis=1, tiled=True),
        lax.all_gather(out_weight, "ctx", axis=1, tiled=True),
        lax.all_gather(gate_up_weight, "ctx", axis=1, tiled=True),
        lax.all_gather(down_weight, "ctx", axis=1, tiled=True),
        lax.all_gather(norm_gains, "ctx", axis=1, tiled=True),
    )
    n_ctx = lax.axis_size("ctx")
    tok_group = block_input.shape[0] * lax.axis_size("tp")
    n_tokens = tok_group * n_ctx
    local_width = qkv_full.shape[2]
    heads_here = local_width // HD
    score_scale = HD ** (-0.5)
    own_pos = lax.dynamic_slice_in_dim(positions, lax.axis_index("ctx") * tok_group, tok_group, 0)
    cos_tab, sin_tab = rope_tables(own_pos, HD)
    attention_norm_gain = gains_full[0].astype(jnp.float32)
    perceptron_norm_gain = gains_full[1].astype(jnp.float32)
    input_single_precision = block_input.astype(jnp.float32)
    attention_root_mean_square = inv_rms(input_single_precision)
    attention_unit_rows = input_single_precision * attention_root_mean_square
    attention_normed_rows = (attention_unit_rows * attention_norm_gain).astype(jnp.bfloat16)
    rows_attn = lax.all_gather(attention_normed_rows, "tp", axis=0, tiled=True)
    projected = jnp.einsum("td,kde->kte", rows_attn, qkv_full, preferred_element_type=jnp.float32)
    query_bf = rotate(projected[0], cos_tab, sin_tab, heads_here, HD).astype(jnp.bfloat16)
    key_bf = rotate(projected[1], cos_tab, sin_tab, heads_here, HD).astype(jnp.bfloat16)
    value_bf = projected[2].astype(jnp.bfloat16)
    key_all, value_all = (
        lax.all_gather(key_bf, "ctx", axis=0, tiled=True),
        lax.all_gather(value_bf, "ctx", axis=0, tiled=True),
    )
    key_block = math.gcd(n_tokens, 2048)
    n_blocks = n_tokens // key_block
    key_stack = key_all.reshape(n_blocks, key_block, heads_here, HD)
    value_stack = value_all.reshape(n_blocks, key_block, heads_here, HD)
    pos_stack = positions.reshape(n_blocks, key_block)
    query_heads = query_bf.reshape(tok_group, heads_here, HD)

    def gather_stats(running, inputs):
        row_peak, row_total = running
        key_blk, pos_blk = inputs
        scores, visible = masked_scores(query_heads, key_blk, own_pos, pos_blk, score_scale)
        new_peak = jnp.maximum(row_peak, jnp.max(scores, axis=-1))
        row_total = row_total * jnp.exp(row_peak - new_peak) + jnp.sum(
            jnp.where(visible, jnp.exp(scores - new_peak[..., None]), 0.0), axis=-1
        )
        return ((new_peak, row_total), None)

    start_stats = (
        jnp.full((heads_here, tok_group), -1e30, jnp.float32),
        jnp.zeros((heads_here, tok_group), jnp.float32),
    )
    (row_peak, row_total), unused = lax.scan(gather_stats, start_stats, (key_stack, pos_stack))
    log_total = row_peak + jnp.log(row_total)

    def mix_values(running, inputs):
        key_blk, value_blk, pos_blk = inputs
        scores, visible = masked_scores(query_heads, key_blk, own_pos, pos_blk, score_scale)
        weights = jnp.where(visible, jnp.exp(scores - log_total[..., None]), 0.0).astype(
            jnp.bfloat16
        )
        return (
            running
            + jnp.einsum("hqk,khd->qhd", weights, value_blk, preferred_element_type=jnp.float32),
            None,
        )

    zero_heads = jnp.zeros((tok_group, heads_here, HD), jnp.float32)
    mixed_heads, unused = lax.scan(mix_values, zero_heads, (key_stack, value_stack, pos_stack))
    attn_bf = mixed_heads.reshape(tok_group, local_width).astype(jnp.bfloat16)
    attn_part = jnp.dot(attn_bf, out_full, preferred_element_type=jnp.float32)
    hidden_residual = input_single_precision + lax.psum_scatter(
        attn_part, "tp", scatter_dimension=0, tiled=True
    )
    perceptron_root_mean_square = inv_rms(hidden_residual)
    perceptron_unit_rows = hidden_residual * perceptron_root_mean_square
    perceptron_normed_rows = (perceptron_unit_rows * perceptron_norm_gain).astype(jnp.bfloat16)
    rows_mlp = lax.all_gather(perceptron_normed_rows, "tp", axis=0, tiled=True)
    gate_up = jnp.einsum("td,kde->kte", rows_mlp, gate_up_full, preferred_element_type=jnp.float32)
    gate_pre = gate_up[0]
    up_pre = gate_up[1]
    sigmoid_gate = jax.nn.sigmoid(gate_pre)
    activated = gate_pre * sigmoid_gate
    hidden_bf = (activated * up_pre).astype(jnp.bfloat16)
    mlp_part = jnp.dot(hidden_bf, down_full, preferred_element_type=jnp.float32)
    block_output = (
        hidden_residual
        + lax.psum_scatter(
            mlp_part.astype(jnp.bfloat16), "tp", scatter_dimension=0, tiled=True
        ).astype(jnp.float32)
    ).astype(jnp.bfloat16)
    grad_rows = lax.all_gather(layer_output_gradient, "tp", axis=0, tiled=True)
    down_grad = jnp.einsum("tf,td->fd", hidden_bf, grad_rows, preferred_element_type=jnp.float32)
    hidden_grad = jnp.einsum("td,fd->tf", grad_rows, down_full, preferred_element_type=jnp.float32)
    gate_grad_bf = (
        hidden_grad * up_pre * (sigmoid_gate * (1.0 + gate_pre * (1.0 - sigmoid_gate)))
    ).astype(jnp.bfloat16)
    up_grad_bf = (hidden_grad * activated).astype(jnp.bfloat16)
    branch_grads = jnp.stack([gate_grad_bf, up_grad_bf])
    gate_up_grad = jnp.einsum(
        "td,kte->kde", rows_mlp, branch_grads, preferred_element_type=jnp.float32
    )
    normed_part_mlp = jnp.einsum(
        "kte,kde->td", branch_grads, gate_up_full, preferred_element_type=jnp.float32
    )
    perceptron_normed_gradient = lax.psum_scatter(
        normed_part_mlp.astype(jnp.bfloat16), "tp", scatter_dimension=0, tiled=True
    ).astype(jnp.float32)
    perceptron_unit_gradient = perceptron_normed_gradient * perceptron_norm_gain
    perceptron_gain_gradient = jnp.sum(perceptron_normed_gradient * perceptron_unit_rows, axis=0)
    residual_stream_gradient = layer_output_gradient.astype(
        jnp.float32
    ) + perceptron_root_mean_square * (
        perceptron_unit_gradient
        - perceptron_unit_rows
        * jnp.mean(perceptron_unit_gradient * perceptron_unit_rows, axis=-1, keepdims=True)
    )
    branch_rows = lax.all_gather(
        residual_stream_gradient.astype(jnp.bfloat16), "tp", axis=0, tiled=True
    )
    out_weight_grad = jnp.einsum(
        "te,td->ed", attn_bf, branch_rows, preferred_element_type=jnp.float32
    )
    attn_grad_bf = jnp.einsum(
        "td,ed->te", branch_rows, out_full, preferred_element_type=jnp.float32
    ).astype(jnp.bfloat16)
    attn_heads = attn_bf.reshape(tok_group, heads_here, HD)
    attn_grad_heads = attn_grad_bf.reshape(tok_group, heads_here, HD)
    deltas = jnp.einsum(
        "qhd,qhd->hq", attn_grad_heads, attn_heads, preferred_element_type=jnp.float32
    )

    def back_block(query_grad, inputs):
        key_blk, value_blk, pos_blk = inputs
        query_part, key_part, value_part = block_grads(
            query_heads,
            attn_grad_heads,
            log_total,
            deltas,
            own_pos,
            key_blk,
            value_blk,
            pos_blk,
            score_scale,
        )
        terms = jnp.concatenate(
            [key_part.reshape(key_block, local_width), value_part.reshape(key_block, local_width)],
            axis=1,
        )
        return (query_grad + query_part, terms)

    query_grad, term_stack = lax.scan(back_block, zero_heads, (key_stack, value_stack, pos_stack))
    own_terms = lax.psum_scatter(
        term_stack.reshape(n_tokens, 2 * local_width).astype(jnp.bfloat16),
        "ctx",
        scatter_dimension=0,
        tiled=True,
    ).astype(jnp.float32)
    key_grad = own_terms[:, :local_width]
    value_grad = own_terms[:, local_width:]
    query_raw = unrotate(
        query_grad.reshape(tok_group, local_width), cos_tab, sin_tab, heads_here, HD
    ).astype(jnp.bfloat16)
    key_raw = unrotate(key_grad, cos_tab, sin_tab, heads_here, HD).astype(jnp.bfloat16)
    value_raw = value_grad.astype(jnp.bfloat16)
    proj_grads = jnp.stack([query_raw, key_raw, value_raw])
    qkv_grad = jnp.einsum("td,kte->kde", rows_attn, proj_grads, preferred_element_type=jnp.float32)
    normed_part_attn = jnp.einsum(
        "kte,kde->td", proj_grads, qkv_full, preferred_element_type=jnp.float32
    )
    attention_normed_gradient = lax.psum_scatter(
        normed_part_attn.astype(jnp.bfloat16), "tp", scatter_dimension=0, tiled=True
    ).astype(jnp.float32)
    attention_unit_gradient = attention_normed_gradient * attention_norm_gain
    attention_gain_gradient = jnp.sum(attention_normed_gradient * attention_unit_rows, axis=0)
    layer_input_gradient = residual_stream_gradient + attention_root_mean_square * (
        attention_unit_gradient
        - attention_unit_rows
        * jnp.mean(attention_unit_gradient * attention_unit_rows, axis=-1, keepdims=True)
    )
    qkv_part, out_part, gate_up_part, down_part = (
        lax.psum_scatter(
            qkv_grad.astype(jnp.bfloat16), "ctx", scatter_dimension=1, tiled=True
        ).astype(jnp.float32),
        lax.psum_scatter(
            out_weight_grad.astype(jnp.bfloat16), "ctx", scatter_dimension=1, tiled=True
        ).astype(jnp.float32),
        lax.psum_scatter(
            gate_up_grad.astype(jnp.bfloat16), "ctx", scatter_dimension=1, tiled=True
        ).astype(jnp.float32),
        lax.psum_scatter(
            down_grad.astype(jnp.bfloat16), "ctx", scatter_dimension=1, tiled=True
        ).astype(jnp.float32),
    )
    gain_part = lax.psum_scatter(
        jnp.stack([attention_gain_gradient, perceptron_gain_gradient]),
        ("ctx", "tp"),
        scatter_dimension=1,
        tiled=True,
    )
    return (
        block_output,
        layer_input_gradient,
        qkv_part,
        out_part,
        gate_up_part,
        down_part,
        gain_part,
    )


def solution(mesh):
    placed = (
        P(("ctx", "tp"), None),
        P(None, "ctx", "tp"),
        P("tp", "ctx"),
        P(None, "ctx", "tp"),
        P("tp", "ctx"),
        P(None, "ctx"),
        P(),
        P(("ctx", "tp"), None),
    )
    return jax.shard_map(
        body,
        mesh=mesh,
        in_specs=placed,
        out_specs=(
            P(("ctx", "tp"), None),
            P(("ctx", "tp"), None),
            P(None, "ctx", "tp"),
            P("tp", "ctx"),
            P(None, "ctx", "tp"),
            P("tp", "ctx"),
            P(None, ("ctx", "tp")),
        ),
        check_vma=False,
    )
```

profile of v0, /device:TPU:0, one launch (start us, length us, event | category | flops | bytes accessed | tf_op | source)
XLA Modules:
  0.0 1754.9 jit_solution(5498511664497382354)
XLA Ops:
  8.3 22.6 %all_gather.33 = bf16[2,2048]{1,0:T(2,128)(2,1)S(1)} all-gather(bf16[2,256]{1,0:T(2,128)(2,1)} %param.13), channel_id=1, replica_groups=mesh['ctx'=8,'tp'=4] {'ctx'}, dimensions={1}, use_global_device_ids=true | all-gather | bytes 9216 | tf_op jit(solution)/shard_map/all_gather | solution.py:88
  33.5 13.3 all-gather.12.cloned.1.call-done
  46.8 100.9 %all-gather.14.cloned.1.call-done = bf16[3,2048,512]{2,1,0:T(8,128)(2,1)} async-done(((bf16[3,256,512]{2,1,0:T(8,128)(2,1)}), bf16[3,2048,512]{2,1,0:T(8,128)(2,1)}) %all-gather.14.cloned.1.call-update) | async-done | bytes 6291472 | tf_op jit(solution)/shard_map/all_gather | solution.py:84
  159.5 41.3 %all-gather.30.cloned.1.call-done = bf16[1,2048,512]{2,1,0:T(8,128)(2,1)} async-done(((bf16[1,256,512]{2,1,0:T(8,128)(2,1)}), bf16[1,2048,512]{2,1,0:T(8,128)(2,1)}) %all-gather.30.cloned.1.call-update) | async-done | bytes 2097168 | tf_op jit(solution)/shard_map/all_gather | solution.py:111
  203.8 48.4 %all-gather.16.cloned.1.call-done = bf16[2048,512]{0,1:T(8,128)(2,1)} async-done(((bf16[256,512]{0,1:T(8,128)(2,1)}), bf16[2048,512]{0,1:T(8,128)(2,1)}) %all-gather.16.cloned.1.call-update) | async-done | bytes 2097168 | tf_op jit(solution)/shard_map/all_gather | solution.py:110
  267.7 35.0 %all-gather.18.cloned.1.call-done = bf16[512,2048]{1,0:T(8,128)(2,1)} async-done(((bf16[512,256]{1,0:T(8,128)(2,1)}), bf16[512,2048]{1,0:T(8,128)(2,1)}) %all-gather.18.cloned.1.call-update) | async-done | bytes 2097168 | tf_op jit(solution)/shard_map/all_gather | solution.py:85
  306.4 29.4 %reduce-scatter.13.cloned.1.call-done = f32[64,2048]{1,0:T(8,128)} async-done(((f32[256,2048]{1,0:T(8,128)}), f32[64,2048]{1,0:T(8,128)}) %reduce-scatter.13.cloned.1.call-update) | async-done | bytes 524304 | tf_op jit(solution)/shard_map/reduce_scatter | solution.py:153
  340.3 14.6 all-gather.20.cloned.1.call-done
  354.8 229.5 %all-gather.22.cloned.1.call-done = bf16[2,2048,2048]{2,1,0:T(8,128)(2,1)} async-done(((bf16[2,256,2048]{2,1,0:T(8,128)(2,1)}), bf16[2,2048,2048]{2,1,0:T(8,128)(2,1)}) %all-gather.22.cloned.1.call-update) | async-done | bytes 16777232 | tf_op jit(solution)/shard_map/all_gather | solution.py:86
  584.3 12.7 convolution_bitcast_fusion
  600.8 126.9 %all-gather.24.cloned.1.call-done = bf16[2048,2048]{1,0:T(8,128)(2,1)} async-done(((bf16[2048,256]{1,0:T(8,128)(2,1)}), bf16[2048,2048]{1,0:T(8,128)(2,1)}) %all-gather.24.cloned.1.call-update) | async-done | bytes 8388624 | tf_op jit(solution)/shard_map/all_gather | solution.py:87
  736.9 12.0 fusion.2
  748.9 23.0 %reduce-scatter.17.cloned.1.call-done = bf16[64,2048]{1,0:T(8,128)(2,1)} async-done(((bf16[256,2048]{1,0:T(8,128)(2,1)}), bf16[64,2048]{1,0:T(8,128)(2,1)}) %reduce-scatter.17.cloned.1.call-update) | async-done | bytes 262160 | tf_op jit(solution)/shard_map/reduce_scatter | solution.py:187
  775.9 16.6 all-gather.28.cloned.1.call-done
  795.4 10.4 convolution_convert_fusion.2
  805.7 11.1 multiply_convert_fusion
  838.7 81.3 %reduce-scatter.19.cloned.1.call-done = bf16[256,1024]{1,0:T(8,128)(2,1)} async-done(((bf16[2048,1024]{1,0:T(8,128)(2,1)}), bf16[256,1024]{1,0:T(8,128)(2,1)}) %reduce-scatter.19.cloned.1.call-update) | async-done | bytes 524304 | tf_op jit(solution)/shard_map/reduce_scatter | solution.py:234
  939.3 13.9 reduce-scatter.21.cloned.1.call-done
  979.2 47.2 %reduce-scatter.25.cloned.1.call-done = bf16[512,256]{1,0:T(8,128)(2,1)} async-done(((bf16[512,2048]{1,0:T(8,128)(2,1)}), bf16[512,256]{1,0:T(8,128)(2,1)}) %reduce-scatter.25.cloned.1.call-update) | async-done | bytes 262160 | tf_op jit(solution)/shard_map/reduce_scatter | solution.py:266
  1028.2 24.4 %reduce-scatter.15.cloned.1.call-done = bf16[64,2048]{1,0:T(8,128)(2,1)} async-done(((bf16[256,2048]{1,0:T(8,128)(2,1)}), bf16[64,2048]{1,0:T(8,128)(2,1)}) %reduce-scatter.15.cloned.1.call-update) | async-done | bytes 262160 | tf_op jit(solution)/shard_map/reduce_scatter | solution.py:169
  1054.7 137.1 %reduce-scatter.31.cloned.1.call-done = f32[64,2]{1,0:T(8,128)} async-done(((f32[2048,2]{1,0:T(8,128)}), f32[64,2]{1,0:T(8,128)}) %reduce-scatter.31.cloned.1.call-update) | async-done | bytes 528
  1193.2 146.0 %reduce-scatter.29.cloned.1.call-done = bf16[2048,256]{1,0:T(8,128)(2,1)} async-done(((bf16[2048,2048]{1,0:T(8,128)(2,1)}), bf16[2048,256]{1,0:T(8,128)(2,1)}) %reduce-scatter.29.cloned.1.call-update) | async-done | bytes 1048592 | tf_op jit(solution)/shard_map/reduce_scatter | solution.py:272
  1341.9 118.4 %reduce-scatter.23.cloned.1.call-done = bf16[3,256,512]{1,2,0:T(8,128)(2,1)} async-done(((bf16[3,2048,512]{1,2,0:T(8,128)(2,1)}), bf16[3,256,512]{1,2,0:T(8,128)(2,1)}) %reduce-scatter.23.cloned.1.call-update) | async-done | bytes 786448 | tf_op jit(solution)/shard_map/reduce_scatter | solution.py:263
  1462.9 280.6 %reduce-scatter.27.cloned.1.call-done = bf16[2,256,2048]{1,2,0:T(8,128)(2,1)} async-done(((bf16[2,2048,2048]{1,2,0:T(8,128)(2,1)}), bf16[2,256,2048]{1,2,0:T(8,128)(2,1)}) %reduce-scatter.27.cloned.1.call-update) | async-done | bytes 2097168 | tf_op jit(solution)/shard_map/reduce_scatter | solution.py:269
  (164 shorter events, 143.1 us)
Async XLA Ops:
  7.2 39.7 %all-gather.12.cloned.1.call-start = ((), (), s32[]{:S(2)}) async-start(), calls=%async_computation.10 | async-start | bytes 1310720 | tf_op jit(solution)/shard_map/all_gather | solution.py:104
  32.7 115.0 %all-gather.14.cloned.1.call-start = ((), (), s32[]{:S(2)}) async-start(), calls=%async_computation.11 | async-start | bytes 7077888 | tf_op jit(solution)/shard_map/all_gather | solution.py:84
  33.5 167.4 %all-gather.30.cloned.1.call-start = ((), (), s32[]{:S(2)}) async-start(), calls=%async_computation.28 | async-start | bytes 2359296 | tf_op jit(solution)/shard_map/all_gather | solution.py:111
  153.4 98.8 %all-gather.16.cloned.1.call-start = ((), (), s32[]{:S(2)}) async-start(), calls=%async_computation.12 | async-start | bytes 2359296 | tf_op jit(solution)/shard_map/all_gather | solution.py:110
  157.1 99.7 %copy-start.10 = (bf16[256,8,32]{0,2,1:T(8,128)(2,1)}, bf16[256,8,32]{0,2,1:T(8,128)(2,1)S(1)}, u32[]{:S(2)}) copy-start(bf16[256,8,32]{0,2,1:T(8,128)(2,1)S(1)} %get-tuple-element.124) | copy-start | bytes 393220
  157.8 144.9 %all-gather.18.cloned.1.call-start = ((), (), s32[]{:S(2)}) async-start(), calls=%async_computation.13 | async-start | bytes 2359296 | tf_op jit(solution)/shard_map/all_gather | solution.py:85
  158.4 177.5 %reduce-scatter.13.cloned.1.call-start = ((), (), s32[]{:S(2)}) async-start(), calls=%async_computation.14 | async-start | bytes 2621440 | tf_op jit(solution)/shard_map/reduce_scatter | solution.py:153
  306.4 48.4 %all-gather.20.cloned.1.call-start = ((), (), s32[]{:S(2)}) async-start(), calls=%async_computation.15 | async-start | bytes 1310720 | tf_op jit(solution)/shard_map/all_gather | solution.py:159
  337.1 436.6 %copy-start.26 = (f32[64]{0:T(128)}, f32[64]{0:T(128)S(1)}, u32[]{:S(2)}) copy-start(f32[64]{0:T(128)S(1)} %add_rsqrt_fusion) | copy-start | bytes 772
  338.0 246.3 %all-gather.22.cloned.1.call-start = ((), (), s32[]{:S(2)}) async-start(), calls=%async_computation.16 | async-start | bytes 18874368 | tf_op jit(solution)/shard_map/all_gather | solution.py:86
  338.7 262.1 %all-gather.26.cloned.1.call-start = ((), (), s32[]{:S(2)}) async-start(), calls=%async_computation.19 | async-start | bytes 1310720 | tf_op jit(solution)/shard_map/all_gather | solution.py:173
  339.5 388.2 %all-gather.24.cloned.1.call-start = ((), (), s32[]{:S(2)}) async-start(), calls=%async_computation.17 | async-start | bytes 9437184 | tf_op jit(solution)/shard_map/all_gather | solution.py:87
  340.0 431.9 %reduce-scatter.17.cloned.1.call-start = ((), (), s32[]{:S(2)}) async-start(), calls=%async_computation.20 | async-start | bytes 1310720 | tf_op jit(solution)/shard_map/reduce_scatter | solution.py:187
  748.9 43.6 %all-gather.28.cloned.1.call-start = ((), (), s32[]{:S(2)}) async-start(), calls=%async_computation.21 | async-start | bytes 1310720 | tf_op jit(solution)/shard_map/all_gather | solution.py:199
  775.6 144.4 %reduce-scatter.19.cloned.1.call-start = ((), (), s32[]{:S(2)}) async-start(), calls=%async_computation.22 | async-start | bytes 4718592 | tf_op jit(solution)/shard_map/reduce_scatter | solution.py:234
  831.5 89.8 %copy-start.21 = (f32[256,32]{0,1:T(8,128)S(1)}, f32[256,32]{0,1:T(8,128)}, u32[]{:S(2)}) copy-start(f32[256,32]{0,1:T(8,128)} %get-tuple-element.137) | copy-start | bytes 98308
  831.6 89.8 %copy-start.22 = (f32[256,32]{0,1:T(8,128)S(1)}, f32[256,32]{0,1:T(8,128)}, u32[]{:S(2)}) copy-start(f32[256,32]{0,1:T(8,128)} %get-tuple-element.138) | copy-start | bytes 98308
  831.6 121.6 %reduce-scatter.21.cloned.1.call-start = ((), (), s32[]{:S(2)}) async-start(), calls=%async_computation.23 | async-start | bytes 1310720 | tf_op jit(solution)/shard_map/reduce_scatter | solution.py:252
  928.6 97.8 %reduce-scatter.25.cloned.1.call-start = ((), (), s32[]{:S(2)}) async-start(), calls=%async_computation.25 | async-start | bytes 2359296 | tf_op jit(solution)/shard_map/reduce_scatter | solution.py:266
  932.0 120.6 %reduce-scatter.15.cloned.1.call-start = ((), (), s32[]{:S(2)}) async-start(), calls=%async_computation.18 | async-start | bytes 1310720 | tf_op jit(solution)/shard_map/reduce_scatter | solution.py:169
  939.2 252.6 %reduce-scatter.31.cloned.1.call-start = ((), (), s32[]{:S(2)}) async-start(), calls=%async_computation.29 | async-start | bytes 1081344
  955.8 383.3 %reduce-scatter.29.cloned.1.call-start = ((), (), s32[]{:S(2)}) async-start(), calls=%async_computation.27 | async-start | bytes 9437184 | tf_op jit(solution)/shard_map/reduce_scatter | solution.py:272
  961.6 498.7 %reduce-scatter.23.cloned.1.call-start = ((), (), s32[]{:S(2)}) async-start(), calls=%async_computation.24 | async-start | bytes 7077888 | tf_op jit(solution)/shard_map/reduce_scatter | solution.py:263
  968.4 775.0 %reduce-scatter.27.cloned.1.call-start = ((), (), s32[]{:S(2)}) async-start(), calls=%async_computation.26 | async-start | bytes 18874368 | tf_op jit(solution)/shard_map/reduce_scatter | solution.py:269
  (28 other events, 707.3 us)
Sparse Core Ops, SparseCore 0:
  32.9 13.9 all-gather.11
  49.0 98.6 all-gather.13
  153.6 47.2 all-gather.29
  203.3 48.8 all-gather.15
  254.1 48.5 all-gather.17
  306.5 29.3 reduce-scatter.12
  338.1 16.6 all-gather.19
  357.0 227.2 all-gather.21
  585.9 14.8 all-gather.25
  602.7 124.9 all-gather.23
  749.0 22.9 reduce-scatter.16
  775.7 16.6 all-gather.27
  831.7 88.2 reduce-scatter.18
  928.7 24.3 reduce-scatter.20
  957.1 69.2 reduce-scatter.24
  1028.8 23.7 reduce-scatter.14
  1055.3 136.5 reduce-scatter.30
  1195.3 143.8 reduce-scatter.28
  1342.8 117.5 reduce-scatter.22
  1464.0 279.4 reduce-scatter.26
where the time goes:
time: 1760 us; the launch traced here: 1750 us
  waiting for transfers between devices  1530 us (87%)
  matrix products  121 us (7%)
  other arithmetic  33.6 us (2%)
  local copies, waits for them, and re-layouts  25.5 us (1%)
  blocking collectives  22.6 us (1%)
    reduce_scatter x1, waiting for transfers between devices, body(): lax.psum_scatter(gate_up_grad.astype(jnp.bfloat16), 'ctx', scatter_dimens...  281 us
    all_gather x1, waiting for transfers between devices, body(): lax.all_gather(gate_up_weight, 'ctx', axis=1, tiled=True)  229 us
    reduce_scatter x1, waiting for transfers between devices, body(): lax.psum_scatter(down_grad.astype(jnp.bfloat16), 'ctx', scatter_dimension...  146 us
    unnamed x21, waiting for transfers between devices  140 us
    all_gather x1, waiting for transfers between devices, body(): lax.all_gather(down_weight, 'ctx', axis=1, tiled=True)  127 us
    reduce_scatter x1, waiting for transfers between devices, body(): lax.psum_scatter(qkv_grad.astype(jnp.bfloat16), 'ctx', scatter_dimension=...  118 us
    all_gather x1, waiting for transfers between devices, body(): lax.all_gather(qkv_weight, 'ctx', axis=1, tiled=True)  101 us
    reduce_scatter x1, waiting for transfers between devices, body(): lax.psum_scatter(term_stack.reshape(n_tokens, 2 * local_width).astype(jnp...  81.3 us
  transfers between devices with their start and end apart: 20, of which 20 were waited for; matrix products, arithmetic and copies ran while one was open for 5% of the time, Pallas kernels for 0%

commit v1 on v0

v1 whole, which is shorter than its diff:
```python
import functools
import math

import jax
import jax.numpy as jnp
from jax import lax
from jax.experimental import pallas as pl
from jax.experimental.pallas import tpu as pltpu
from jax.sharding import PartitionSpec as P

HD = 64
MESH = pl.DeviceIdType.MESH
DMA = pltpu.SemaphoreType.DMA
ANY = pl.BlockSpec(memory_space=pl.ANY)
VMEM = pl.BlockSpec(memory_space=pltpu.VMEM)
bf16 = jnp.bfloat16
f32 = jnp.float32

norm_eps = 1e-05
rope_base = 130000.0


def inv_rms(values):
    return lax.rsqrt(jnp.mean(values * values, axis=-1, keepdims=True) + norm_eps)


def rope_tables(where_at, head_dim):
    half_dim = head_dim // 2
    inv_freq = rope_base ** (-(jnp.arange(half_dim, dtype=f32) * 2.0 / head_dim))
    angles = where_at.astype(f32)[:, None] * inv_freq[None, :]
    return (jnp.cos(angles)[:, None, :], jnp.sin(angles)[:, None, :])


def rotate(values, cos_tab, sin_tab, n_heads, head_dim):
    shaped = values.reshape(values.shape[0], n_heads, head_dim)
    half_dim = head_dim // 2
    lower_half, upper_half = (shaped[..., :half_dim], shaped[..., half_dim:])
    turned = jnp.concatenate(
        [lower_half * cos_tab - upper_half * sin_tab, upper_half * cos_tab + lower_half * sin_tab],
        axis=-1,
    )
    return turned.reshape(values.shape[0], n_heads * head_dim)


def unrotate(values, cos_tab, sin_tab, n_heads, head_dim):
    return rotate(values, cos_tab, -sin_tab, n_heads, head_dim)


class Place:
    def __init__(self, nz):
        ctx, tp = lax.axis_index("ctx"), lax.axis_index("tp")
        self.nz = nz
        self.first = ctx // (2 * nz) * (2 * nz)
        self.z, self.y = (ctx - self.first) // 2, (ctx - self.first) % 2
        self.x, self.k = tp // 2, tp % 2

    def device(self, z, y, x, k):
        return {"ctx": self.first + 2 * z + y, "tp": 2 * x + k}


def slot_of(z, x, k):
    return (z * 2 + x) * 2 + k


class Comm:
    def __init__(self, at, pool):
        self.at, self.pool, self.used, self.ends, self.late = at, pool, 0, [], []
        z, y, x, k, nz = at.z, at.y, at.x, at.k, at.nz
        self.to_x = at.device(z, y, 1 - x, k)
        self.to_k = at.device(z, y, x, 1 - k)
        self.to_y = at.device(z, 1 - y, x, k)
        self.to_xk = at.device(z, y, 1 - x, 1 - k)
        peers = [self.to_x, self.to_k, self.to_y, self.to_xk]
        peers += [at.device((z + d) % nz, y, x, k) for d in range(1, nz)]
        barrier = pltpu.get_barrier_semaphore()
        for peer in peers:
            pl.semaphore_signal(barrier, inc=1, device_id=peer, device_id_type=MESH)
        pl.semaphore_wait(barrier, len(peers))

    def sem(self):
        self.used += 1
        return self.pool.at[self.used - 1]

    def sems(self, n):
        return [self.sem() for _ in range(n)]

    def step(self, arrivals, copies, cond=None, then=None):
        sems = self.sems(len(copies))

        def copy(i):
            src, dst, recv_sem, device = copies[i]
            return pltpu.make_async_remote_copy(
                src_ref=src,
                dst_ref=dst,
                send_sem=sems[i],
                recv_sem=recv_sem,
                device_id=device,
                device_id_type=MESH,
            )

        def go():
            for buf, sem in arrivals:
                self.arrive(buf, sem)
            if then is not None:
                then()
            for i in range(len(copies)):
                copy(i).start()

        def end():
            for i in range(len(copies)):
                copy(i).wait_send()

        if cond is None:
            go()
        else:
            pl.when(cond)(go)
        if copies:
            self.ends.append((cond, end))

    def keep(self, src, dst):
        copy = pltpu.make_async_copy(src, dst, self.sem())
        copy.start()
        self.ends.append((None, copy.wait))

    def arrive(self, buf, recv_sem):
        pltpu.make_async_remote_copy(
            src_ref=buf,
            dst_ref=buf,
            send_sem=recv_sem,
            recv_sem=recv_sem,
            device_id=self.to_k,
            device_id_type=MESH,
        ).wait_recv()

    def finish(self):
        for buf, sem in self.late:
            self.arrive(buf, sem)
        for cond, end in self.ends:
            if cond is None:
                end()
            else:
                pl.when(cond)(end)


def take_turns(*steps):
    steps = list(steps)
    while steps:
        for one in list(steps):
            if next(one, steps) is steps:
                steps.remove(one)


def advance(steps, n):
    for _ in range(n):
        next(steps, None)


def exhaust(*many):
    for steps in many:
        for _ in steps:
            pass


def line(at):
    places = []
    for d in range(1, at.nz):
        places.append((d, -1, (at.z + at.nz - d) % at.nz, at.z >= d))
        places.append((d, 1, (at.z + d) % at.nz, at.z + d < at.nz))
    return places


def z_steps(at):
    return 2 * at.nz - 1


def gather_steps(comm, own, o_ref, lo, size):
    at = comm.at
    z, x, k, nz = at.z, at.x, at.k, at.nz
    rows = own.shape[0]
    places = [(0, 0, z, None)] + line(at)
    n = len(places)
    sem_z, sem_x, sem_k = (comm.sems(m * n) for m in (1, 1, 2))

    def part(slot):
        return o_ref.at[pl.ds(pl.multiple_of(slot * rows + lo, size), size), :]

    for i, (d, side, zi, cond) in enumerate(places):
        slot = slot_of(zi, x, k)
        here = own.at[pl.ds(lo, size), :] if d == 0 else part(slot)
        if d:
            comm.step([(part(slot), sem_z[i])], [], cond)
        for way in (1, -1):
            if d < nz - 1 and side != way:
                on = (z < nz - 1) if way == 1 else (z > 0)
                if cond is not None:
                    on = on & cond
                to = at.device((z + nz + way) % nz, at.y, x, k)
                j = next(j for j, p in enumerate(places) if p[0] == d + 1 and p[1] == -way)
                comm.step([], [(here, part(slot), sem_z[j], to)], on)
        comm.step(
            [],
            [
                (here, part(slot), sem_x[i], comm.to_x),
                (here, part(slot), sem_k[i], comm.to_k),
            ],
            cond,
        )
        if d == 0:
            comm.keep(here, part(slot))
        yield
    for i, (d, side, zi, cond) in enumerate(places):
        slot = slot_of(zi, 1 - x, k)
        comm.step(
            [(part(slot), sem_x[i])], [(part(slot), part(slot), sem_k[n + i], comm.to_k)], cond
        )
        yield
    for h, xh in enumerate((x, 1 - x)):
        for i, (d, side, zi, cond) in enumerate(places):
            comm.step([(part(slot_of(zi, xh, 1 - k)), sem_k[h * n + i])], [], cond)


def add_rows(dst, terms):
    rows = dst.shape[0]
    step = math.gcd(rows, 16)

    def some_rows(i, _):
        r = pl.ds(pl.multiple_of(i * step, step), step)
        total = terms[0][r, :].astype(f32)
        for term in terms[1:]:
            total = total + term[r, :].astype(f32)
        dst[r, :] = total.astype(dst.dtype)
        return 0

    lax.fori_loop(0, rows // step, some_rows, 0)


def far_first(at):
    nz = at.nz
    orders = []
    for z in range(nz):
        others = sorted((c for c in range(nz) if c != z), key=lambda c: (-abs(c - z), c))
        orders.append([(abs(c - z), 1 if c > z else -1, c) for c in others] + [(0, 0, z)])
    here = [1 - ((at.z - c) * (at.z - c) + nz * nz - 1) // (nz * nz) for c in range(nz)]
    return [
        tuple(sum(here[c] * orders[c][t][i] for c in range(nz)) for i in range(3))
        for t in range(nz)
    ]


class Scatter:
    def __init__(self, comm, p_ref, bufs, total):
        nz = comm.at.nz
        self.comm, self.p_ref, self.bufs, self.total = comm, p_ref, bufs, total
        self.targets = far_first(comm.at)
        self.sem_k, self.sem_x = comm.sems(2 * nz), comm.sems(nz)
        self.sem_z = comm.used
        comm.sems(2 * nz)

    def mine(self, zi, flip, core):
        x = self.comm.at.x
        return self.p_ref.at[slot_of(zi, 1 - x if flip else x, core)]

    def passing(self, side, d):
        i = (side + 1) // 2 * self.comm.at.nz + d
        return self.bufs[2].at[i], self.comm.pool.at[self.sem_z + i]

    def first(self, t):
        comm, nz, k = self.comm, self.comm.at.nz, self.comm.at.k
        zi = self.targets[t][2]
        comm.step(
            [],
            [
                (self.mine(zi, flip, 1 - k), self.bufs[0].at[flip * nz + zi],
                 self.sem_k[flip * nz + t], comm.to_k)
                for flip in (1, 0)
            ],
        )

    def second(self, t):
        comm, nz, k = self.comm, self.comm.at.nz, self.comm.at.k
        zi = self.targets[t][2]
        b = self.bufs[0].at[nz + zi]
        comm.step(
            [(b, self.sem_k[nz + t])],
            [(b, self.bufs[1].at[zi], self.sem_x[t], comm.to_x)],
            None,
            lambda: add_rows(b, [b, self.mine(zi, 1, k)]),
        )

    def third(self, t):
        comm, at = self.comm, self.comm.at
        z, nz, k = at.z, at.nz, at.k
        d, side, zi = self.targets[t]
        b, landed = self.bufs[0].at[zi], self.bufs[1].at[zi]
        terms = [b, self.mine(zi, 0, k), landed]
        comm.arrive(b, self.sem_k[t])
        comm.arrive(landed, self.sem_x[t])
        if t == nz - 1:
            add_rows(self.total, terms)
            for way, on in ((1, z > 0), (-1, z < nz - 1)):
                buf, sem = self.passing(way, 0)

                @pl.when(on)
                def _():
                    comm.arrive(buf, sem)
                    add_rows(self.total, [self.total, buf])

            return
        add_rows(b, terms)
        buf, sem = self.passing(side, d)
        behind = z - side

        @pl.when((behind >= 0) & (behind < nz))
        def _():
            comm.arrive(buf, sem)
            add_rows(b, [b, buf])

        dst, sem = self.passing(side, d - 1)
        comm.step([], [(b, dst, sem, at.device(z + side, at.y, at.x, k))])

    def steps(self, produce=None):
        nz = self.comm.at.nz
        for i in range(nz + 2):
            if i < nz:
                if produce is not None:
                    produce(self.targets[i][2])
                self.first(i)
            yield
            for stage, lag in ((self.second, 1), (self.third, 2)):
                if 0 <= i - lag < nz:
                    stage(i - lag)
                    yield


def scatter_bufs(nz, rows, width):
    return [pltpu.VMEM((n * nz, rows, width), bf16) for n in (2, 1, 2)]


def along(ref, axis, i, size):
    r = pl.ds(pl.multiple_of(i * size, size), size)
    before = (slice(None),) * (len(ref.shape) - axis)
    return ref.at[before + (r,) + (slice(None),) * (axis - 1)]


class Swap:
    def __init__(self, array, unit_axis, feature_axis, units, depth, shape, plane=None):
        self.array, self.shape, self.plane = array, shape, plane
        self.unit_axis, self.feature_axis, self.units, self.depth = unit_axis, feature_axis, units, depth
        self.out = jax.ShapeDtypeStruct(shape, bf16)

    def of_units(self, ref, z):
        if self.plane is not None:
            ref = ref.at[self.plane]
        return along(ref, self.unit_axis, z, self.units)

    def of_features(self, ref, z, y):
        return along(ref, self.feature_axis, 2 * z + y, self.depth)


def swap_in(comm, swaps, srcs, dsts):
    at = comm.at
    z, y, x, k, nz = at.z, at.y, at.x, at.k, at.nz
    sem_z = [comm.sems(nz) for _ in swaps]
    sem_y = [comm.sems(nz) for _ in swaps]

    def sends():
        for i, one in enumerate(swaps):
            mine = one.of_features(dsts[i], z, y)
            for d in range(1, nz):
                zi = (z + d) % nz
                comm.step([], [(one.of_units(srcs[i], zi), mine, sem_z[i][d], at.device(zi, y, x, k))])
                yield
            own = one.of_units(srcs[i], z)
            comm.step([], [(own, mine, sem_y[i][0], comm.to_y)])
            comm.keep(own, mine)
            yield

    def passes():
        for i, one in enumerate(swaps):
            for d in range(1, nz):
                come = one.of_features(dsts[i], (z + nz - d) % nz, y)
                comm.step([(come, sem_z[i][d])], [(come, come, sem_y[i][d], comm.to_y)])
                yield
        for i, one in enumerate(swaps):
            for d in range(nz):
                zi = (z + nz - d) % nz
                comm.late.append((one.of_features(dsts[i], zi, 1 - y), sem_y[i][d]))

    return sends(), passes()


def add_piece(dst, src):
    if len(dst.shape) == 3:
        for p in range(dst.shape[0]):
            add_rows(dst.at[p], [dst.at[p], src.at[p]])
    else:
        add_rows(dst, [dst, src])


def swap_out(comm, swaps, srcs, dsts, landed):
    at = comm.at
    z, y, x, k, nz = at.z, at.y, at.x, at.k, at.nz
    sem_y = [comm.sems(nz) for _ in swaps]
    sem_z = [comm.sems(nz) for _ in swaps]

    def sends():
        for i, one in enumerate(swaps):
            for d in list(range(1, nz)) + [0]:
                zi = (z + d) % nz
                comm.step(
                    [], [(one.of_features(srcs[i], zi, 1 - y), landed[i].at[zi], sem_y[i][d], comm.to_y)]
                )
                yield

    def passes():
        for i, one in enumerate(swaps):
            mine = one.of_units(dsts[i], z)
            for d in list(range(1, nz)) + [0]:
                zi = (z + d) % nz
                buf = landed[i].at[zi]
                comm.arrive(buf, sem_y[i][d])
                add_piece(buf, one.of_features(srcs[i], zi, y))
                if d:
                    comm.step([], [(buf, mine, sem_z[i][d], at.device(zi, y, x, k))])
                else:
                    comm.keep(buf, mine)
                yield
        for i, one in enumerate(swaps):
            for d in range(1, nz):
                comm.late.append((one.of_units(dsts[i], (z + nz - d) % nz), sem_z[i][d]))

    return sends(), passes()


def landing(nz, one, user_shape):
    shape = list(user_shape)
    shape[len(shape) - one.feature_axis] = one.depth
    return pltpu.VMEM((nz, *shape), bf16)


def comm_kernel(nz, work, swaps, n_in, n_out, *refs):
    given = [one for one in swaps if one.array is not None]
    m, g = len(swaps), len(given)
    ins, srcs = refs[:n_in], refs[n_in : n_in + g]
    outs = refs[n_in + g : n_in + g + n_out]
    dsts = refs[n_in + g + n_out : n_in + g + n_out + m]
    scratch = refs[n_in + g + n_out + m :]
    comm = Comm(Place(nz), scratch[-1])
    work(comm, (swaps, srcs, dsts), ins, outs, scratch[:-1])
    comm.finish()


def comm_call(name, nz, collective, work, ins, outs, scratch, swaps, swap_spec=ANY, vmem=48):
    given = [one.array for one in swaps if one.array is not None]
    return pl.pallas_call(
        functools.partial(comm_kernel, nz, work, swaps, len(ins), len(outs)),
        out_shape=[jax.ShapeDtypeStruct(s, d) for s, d, _ in outs] + [one.out for one in swaps],
        in_specs=[s for _, s in ins] + [swap_spec] * len(given),
        out_specs=[s for _, _, s in outs] + [ANY] * len(swaps),
        scratch_shapes=scratch + [DMA((600,))],
        compiler_params=pltpu.CompilerParams(
            collective_id=collective, has_side_effects=True, vmem_limit_bytes=vmem * 2**20
        ),
        name=name,
    )(*[v for v, _ in ins], *given)


def by_rows(lo, size, do):
    step = math.gcd(size, 16)

    def some_rows(i, _):
        do(pl.ds(pl.multiple_of(lo + i * step, step), step))
        return 0

    lax.fori_loop(0, size // step, some_rows, 0)


def halves(rows):
    return [(0, rows // 2), (rows // 2, rows // 2)] if rows % 32 == 0 else [(0, rows)]


def feature_pieces(nz, groups, d_model):
    a = 2 * nz
    r = d_model // a // groups
    return [(c, i * r, (i * a + c) * r, r) for c in range(a) for i in range(groups)]


def sum_gains(comm, groups, sums, sorted_sums, landed, total):
    at = comm.at
    z, y, x, k, nz = at.z, at.y, at.x, at.k, at.nz
    for c, lo, col, r in feature_pieces(nz, groups, sums.shape[1]):
        sorted_sums[c % 2, c // 2, :, lo : lo + r] = sums[:, col : col + r]
    sem = comm.sems(4 + nz)
    comm.step([], [(sorted_sums.at[1 - y], landed.at[pl.ds(0, nz)], sem[0], comm.to_y)])
    comm.arrive(landed.at[pl.ds(0, nz)], sem[0])
    sorted_sums[y] += landed[0:nz]
    for d in range(1, nz):
        zi = (z + d) % nz
        comm.step([], [(sorted_sums.at[y, zi], landed.at[nz + d], sem[d], at.device(zi, y, x, k))])
    total[...] = sorted_sums[y, z]
    for d in range(1, nz):
        comm.arrive(landed.at[nz + d], sem[d])
        total[...] += landed[nz + d]
    landed[nz] = total[...]
    for i, to in enumerate((comm.to_k, comm.to_x, comm.to_xk)):
        comm.step([], [(landed.at[nz], landed.at[2 * nz + i], sem[nz + i], to)])
    for i in range(3):
        comm.arrive(landed.at[2 * nz + i], sem[nz + i])
        total[...] += landed[2 * nz + i]


def gains_of_group(comm, groups, gain_ref, landed, gains):
    at = comm.at
    z, y, x, k, nz = at.z, at.y, at.x, at.k, at.nz
    sem = comm.sems(nz + 1)
    for d in range(1, nz):
        to = at.device((z + d) % nz, y, x, k)
        comm.step([], [(gain_ref, landed.at[y, z], sem[d], to)])
    landed[y, z] = gain_ref[...]
    for d in range(1, nz):
        comm.arrive(landed.at[y, (z + nz - d) % nz], sem[d])
    comm.step([], [(landed.at[y], landed.at[y], sem[0], comm.to_y)])
    comm.arrive(landed.at[1 - y], sem[0])
    for c, lo, col, r in feature_pieces(nz, groups, gains.shape[1]):
        gains[:, col : col + r] = landed[c % 2, c // 2, :, lo : lo + r].astype(f32)


def start_work(groups, comm, swap, ins, outs, scratch):
    x_ref, gain_ref = ins
    rows_attn, gains = outs
    normed, landed = scratch
    at = comm.at
    gains_of_group(comm, groups, gain_ref, landed, gains)

    def norm(r):
        x = x_ref[r, :].astype(f32)
        normed[r, :] = (x * inv_rms(x) * gains[0:1, :]).astype(bf16)

    rows = x_ref.shape[0]
    by_rows(0, rows, norm)
    shards = gather_steps(comm, normed, rows_attn, 0, rows)
    sends, passes = swap_in(comm, *swap)
    advance(shards, 1)
    advance(sends, at.nz)
    take_turns(shards, sends)
    exhaust(passes)


def product_into(p_ref, rows, at_slot, lhs, rhs, rhs_dims):
    n = p_ref.shape[2]
    wide = math.gcd(n, 512)
    count = lhs[0].shape[0] // rows
    for j in range(n // wide):
        cols = slice(j * wide, (j + 1) * wide)
        total = None
        for one, right, dims in zip(lhs, rhs, rhs_dims):
            block = right[:, cols] if dims == 0 else right[cols, :]
            term = lax.dot_general(one, block, (((1,), (dims,)), ((), ())), preferred_element_type=f32)
            total = term if total is None else total + term
        p_ref[pl.ds(at_slot, count), :, cols] = total.astype(bf16).reshape(count, rows, wide)


def row_blocks(rows, keys, do):
    step = math.gcd(rows, 128)
    fine = max(16, min(128, 128 * 2048 // keys))
    for i in range(rows // step):

        def some(j, _):
            do(pl.ds(pl.multiple_of(i * step + j * fine, fine), fine))
            return 0

        lax.fori_loop(0, step // fine, some, 0)
        yield


def attend(heads, q_ref, k_ref, v_ref, at_q, at_k, o_ref, lse_ref):
    def block(r):
        visible = at_k[...] <= at_q[r, :]
        for h in range(heads):
            c = slice(h * HD, (h + 1) * HD)
            scores = lax.dot_general(
                q_ref[r, c], k_ref[:, c], (((1,), (1,)), ((), ())), preferred_element_type=f32
            )
            scores = jnp.where(visible, scores, -1e30)
            peak = jnp.max(scores, axis=-1, keepdims=True)
            weights = jnp.exp(scores - peak)
            total = jnp.sum(weights, axis=-1, keepdims=True)
            probs = (weights * (1.0 / total)).astype(bf16)
            o_ref[r, c] = jnp.dot(probs, v_ref[:, c], preferred_element_type=f32).astype(bf16)
            lse_ref[r, h : h + 1] = peak + jnp.log(total)

    yield from row_blocks(q_ref.shape[0], k_ref.shape[0], block)


def attend_back(heads, q_ref, k_ref, v_ref, at_q, at_k, o_ref, lse_ref, do_ref, dq_ref, dk_ref, dv_ref):
    over_rows = (((0,), (0,)), ((), ()))
    over_cols = (((1,), (1,)), ((), ()))
    dk_ref[...] = jnp.zeros_like(dk_ref)
    dv_ref[...] = jnp.zeros_like(dv_ref)

    def block(r):
        visible = at_k[...] <= at_q[r, :]
        for h in range(heads):
            c = slice(h * HD, (h + 1) * HD)
            q, grad = q_ref[r, c], do_ref[r, c]
            scores = lax.dot_general(q, k_ref[:, c], over_cols, preferred_element_type=f32)
            scores = jnp.where(visible, scores, -1e30)
            probs = jnp.exp(scores - lse_ref[r, h : h + 1])
            delta = jnp.sum(
                grad.astype(f32) * o_ref[r, c].astype(f32), axis=-1, keepdims=True
            )
            prob_grad = lax.dot_general(grad, v_ref[:, c], over_cols, preferred_element_type=f32)
            score_grad = (probs * (prob_grad - delta)).astype(bf16)
            dq_ref[r, c] = jnp.dot(score_grad, k_ref[:, c], preferred_element_type=f32) * HD ** (-0.5)
            dk_ref[c, :] += lax.dot_general(q, score_grad, over_rows, preferred_element_type=f32)
            dv_ref[c, :] += lax.dot_general(
                grad, probs.astype(bf16), over_rows, preferred_element_type=f32
            )

    yield from row_blocks(q_ref.shape[0], k_ref.shape[0], block)


def attend_work(heads, comm, swap, ins, outs, scratch):
    q_ref, k_ref, v_ref, at_q, at_k, dy_ref = ins
    o_ref, lse_ref, k_out, v_out, grad_rows = outs
    k_all, v_all = scratch
    at = comm.at
    y, keys = at.y, k_ref.shape[0]

    def half(ref, yy):
        return ref.at[pl.ds(pl.multiple_of(yy * keys, keys), keys), :]

    sem = comm.sems(2)
    for i, (mine, both) in enumerate(((k_ref, k_all), (v_ref, v_all))):
        comm.step([], [(mine, half(both, y), sem[i], comm.to_y)])
        half(both, y)[...] = mine[...]
    grads = gather_steps(comm, dy_ref, grad_rows, 0, dy_ref.shape[0])
    sends, passes = swap_in(comm, *swap)
    advance(grads, 1)
    advance(sends, 4)
    advance(grads, 2)
    for i, (both, out) in enumerate(((k_all, k_out), (v_all, v_out))):
        comm.arrive(half(both, 1 - y), sem[i])
        comm.keep(both, out)
    compute = attend(heads, q_ref, k_all, v_all, at_q, at_k, o_ref, lse_ref)
    take_turns(grads, sends, compute)
    exhaust(passes)


def attend_back_work(heads, comm, swap, ins, outs, scratch):
    q_ref, k_ref, v_ref, at_q, at_k, o_ref, lse_ref, do_ref, p_ref, hidden = ins
    dq_ref, dk_out, dv_out, block_out = outs
    total, dk_ref, dv_ref, going, come, gu_landed = scratch[:6]
    bufs = scratch[6:]
    at = comm.at
    y, keys = at.y, k_ref.shape[0] // 2

    def half(ref, yy):
        return ref.at[:, pl.ds(pl.multiple_of(yy * keys, keys), keys)]

    def out(r):
        block_out[r, :] = (hidden[r, :] + total[r, :]).astype(bf16)

    sends, passes = swap_out(comm, *swap, [gu_landed])
    exhaust(sends)
    steps = Scatter(comm, p_ref, bufs, total).steps()
    compute = attend_back(
        heads, q_ref, k_ref, v_ref, at_q, at_k, o_ref, lse_ref, do_ref, dq_ref, dk_ref, dv_ref
    )
    advance(steps, 2)
    take_turns(compute, steps, passes)
    by_rows(0, hidden.shape[0], out)
    sem = comm.sems(2)
    for i, ref in enumerate((dk_ref, dv_ref)):
        going[i] = half(ref, 1 - y)[...].astype(bf16)
        comm.step([], [(going.at[i], come.at[i], sem[i], comm.to_y)])
    for i, (ref, dst) in enumerate(((dk_ref, dk_out), (dv_ref, dv_out))):
        comm.arrive(come.at[i], sem[i])
        dst[...] = half(ref, y)[...] + come[i].astype(f32)


def middle_work(comm, swap, ins, outs, scratch):
    attn, out_w, x_ref, gains = ins
    hidden, rows_mlp = outs
    normed, p_ref, bufs = scratch[0], scratch[1], scratch[2:]
    rows = x_ref.shape[0]

    def norm(r):
        h = hidden[r, :] + x_ref[r, :].astype(f32)
        hidden[r, :] = h
        normed[r, :] = (h * inv_rms(h) * gains[1:2, :]).astype(bf16)

    def produce(zi):
        r = pl.ds(pl.multiple_of(zi * 4 * rows, 4 * rows), 4 * rows)
        product_into(p_ref, rows, zi * 4, [attn[r, :]], [out_w], [0])

    sends, passes = swap_in(comm, *swap)
    advance(sends, comm.at.nz)
    steps = Scatter(comm, p_ref, bufs, hidden).steps(produce)
    exhaust(steps)
    by_rows(0, rows, norm)
    shards = gather_steps(comm, normed, rows_mlp, 0, rows)
    advance(shards, z_steps(comm.at))
    take_turns(shards, sends, passes)


def norm_back(grad, unit, rms, gain):
    unit_grad = grad * gain
    return rms * (unit_grad - unit * jnp.mean(unit_grad * unit, axis=-1, keepdims=True))


def back_work(groups, comm, swap, ins, outs, scratch):
    rows_mlp, grad_rows, gate_w, up_w, dn_w, hidden, dy_ref, gains = ins
    residual, branch_rows, gain_sum, q_out, gu_out = outs
    total, rounded, p_ref, q_ref, gates, n2, dy, gu_g, dn_g, dn_landed = scratch[:10]
    bufs = scratch[10:]
    at = comm.at
    nz = at.nz
    rows = hidden.shape[0]
    tall = 4 * rows
    gain_sum[...] = jnp.zeros_like(gain_sum)
    sems = comm.sems(2 * nz)

    def load(t, zi):
        r = pl.ds(pl.multiple_of(zi * tall, tall), tall)
        return [
            pltpu.make_async_copy(rows_mlp.at[r, :], n2.at[r, :], sems[2 * t]),
            pltpu.make_async_copy(grad_rows.at[r, :], dy.at[r, :], sems[2 * t + 1]),
        ]

    main = Scatter(comm, p_ref, bufs, total)
    for t in range(nz):
        for copy in load(t, main.targets[t][2]):
            copy.start()
    turn = iter(range(nz))

    def produce(zi):
        for copy in load(next(turn), zi):
            copy.wait()
        r = pl.ds(pl.multiple_of(zi * tall, tall), tall)
        x, g = n2[r, :], dy[r, :]
        gate = jnp.dot(x, gate_w[...], preferred_element_type=f32)
        up = jnp.dot(x, up_w[...], preferred_element_type=f32)
        grad = lax.dot_general(g, dn_w[...], (((1,), (1,)), ((), ())), preferred_element_type=f32)
        sig = jax.nn.sigmoid(gate)
        act = gate * sig
        hid = (act * up).astype(bf16)
        gate_grad = (grad * up * (sig * (1.0 + gate * (1.0 - sig)))).astype(bf16)
        up_grad = (grad * act).astype(bf16)
        gates[0, r, :] = gate_grad
        gates[1, r, :] = up_grad
        gates[2, r, :] = hid
        product_into(p_ref, rows, zi * 4, [gate_grad, up_grad], [gate_w, up_w], [1, 1])
        product_into(q_ref, rows, zi * 4, [hid], [dn_w], [0])

    def back(r):
        h = hidden[r, :]
        rms = inv_rms(h)
        unit, grad = h * rms, total[r, :]
        gain_sum[...] += jnp.sum(grad * unit, axis=0, keepdims=True)
        dh = dy_ref[r, :].astype(f32) + norm_back(grad, unit, rms, gains[1:2, :])
        residual[r, :] = dh
        rounded[r, :] = dh.astype(bf16)

    def gradients():
        d_model = n2.shape[1]
        depth = d_model // (2 * nz)
        over_rows = (((0,), (0,)), ((), ()))
        pieces = feature_pieces(nz, groups, d_model)
        per = max(1, len(pieces) // 8)
        for j in range(0, len(pieces), per):
            for c, lo, col, r in pieces[j : j + per]:
                f, to = slice(col, col + r), slice(c * depth + lo, c * depth + lo + r)
                for p in (0, 1):
                    gu_g[p, to, :] = lax.dot_general(
                        n2[:, f], gates[p], over_rows, preferred_element_type=f32
                    ).astype(bf16)
                dn_g[:, to] = lax.dot_general(
                    gates[2], dy[:, f], over_rows, preferred_element_type=f32
                ).astype(bf16)
            yield

    steps = main.steps(produce)
    others = gradients()
    advance(steps, 3 * nz - 2)
    comm.keep(q_ref, q_out)
    take_turns(steps, others)
    comm.keep(gu_g, gu_out)
    by_rows(0, rows, back)
    shards = gather_steps(comm, rounded, branch_rows, 0, rows)
    sends, passes = swap_out(comm, swap[0], (dn_g,), swap[2], [dn_landed])
    advance(shards, 1)
    exhaust(sends)
    advance(shards, z_steps(at) - 1)
    take_turns(shards, passes)


def last_work(groups, comm, swap, ins, outs, scratch):
    proj_grads, qkv_w, residual, x_ref, gains, gain_sum_2 = ins
    grad_in, gain_out = outs
    total, gain_sums, sorted_sums, landed, qkv_landed, out_landed, p_ref = scratch[:7]
    bufs = scratch[7:]
    rows = x_ref.shape[0]
    gain_sums[0:1, :] = jnp.zeros_like(gain_sum_2)
    gain_sums[1:2, :] = gain_sum_2[...]

    def back(r):
        x = x_ref[r, :].astype(f32)
        rms = inv_rms(x)
        unit, grad = x * rms, total[r, :]
        gain_sums[0:1, :] += jnp.sum(grad * unit, axis=0, keepdims=True)
        grad_in[r, :] = residual[r, :] + norm_back(grad, unit, rms, gains[0:1, :])

    width = qkv_w.shape[2]

    def produce(zi):
        r = pl.ds(pl.multiple_of(zi * 4 * rows, 4 * rows), 4 * rows)
        lhs = [proj_grads[r, p * width : (p + 1) * width] for p in range(3)]
        product_into(p_ref, rows, zi * 4, lhs, [qkv_w.at[p] for p in range(3)], [1] * 3)

    sends, passes = swap_out(comm, *swap, [qkv_landed, out_landed])
    exhaust(sends)
    take_turns(Scatter(comm, p_ref, bufs, total).steps(produce), passes)
    by_rows(0, rows, back)
    sum_gains(comm, groups, gain_sums, sorted_sums, landed, gain_out)


def body(
    block_input,
    qkv_weight,
    out_weight,
    gate_up_weight,
    down_weight,
    norm_gains,
    positions,
    layer_output_gradient,
):
    n_ctx, n_tp = lax.axis_size("ctx"), lax.axis_size("tp")
    nz = math.gcd(qkv_weight.shape[2] // HD, n_ctx // 2)
    nz = math.gcd(nz, 4)
    a = 2 * nz
    b = n_ctx // a
    assert n_tp == 4
    depth = qkv_weight.shape[1] * b
    d_model = depth * a
    width = qkv_weight.shape[2] // nz
    heads = width // HD
    units = down_weight.shape[0] // nz
    rows = block_input.shape[0]
    across = [[i * a + j for i in range(b)] for j in range(a)]

    def over_groups(v, axis):
        return lax.all_gather(v, "ctx", axis=axis, tiled=True, axis_index_groups=across) if b > 1 else v

    def to_groups(v, axis):
        if b == 1:
            return v
        return lax.psum_scatter(
            v, "ctx", scatter_dimension=axis, tiled=True, axis_index_groups=across
        )

    def model_order(v, axis):
        if b == 1:
            return v
        s = v.shape
        w = v.reshape(s[:axis] + (a, b, depth // b) + s[axis + 1 :])
        return jnp.swapaxes(w, axis, axis + 1).reshape(s)

    def swap_order(v, axis):
        if b == 1:
            return v
        s = v.shape
        w = v.reshape(s[:axis] + (b, a, depth // b) + s[axis + 1 :])
        return jnp.swapaxes(w, axis, axis + 1).reshape(s)

    my_gains = over_groups(norm_gains, 1)
    group_rows = 4 * nz * rows
    rows_attn, gains, qkv_w, out_w = comm_call(
        "start", nz, 0, functools.partial(start_work, b),
        [(block_input, VMEM), (my_gains, VMEM)],
        [((group_rows, d_model), bf16, ANY), ((2, d_model), f32, VMEM)],
        [pltpu.VMEM((rows, d_model), bf16), pltpu.VMEM((2, nz) + my_gains.shape, bf16)],
        [Swap(over_groups(qkv_weight, 1), 1, 2, width, depth, (3, d_model, width)),
         Swap(over_groups(out_weight, 1), 2, 1, width, depth, (width, d_model))],
    )
    qkv_w, out_w = model_order(qkv_w, 1), model_order(out_w, 1)

    score_scale = HD ** (-0.5)
    y, group = lax.axis_index("ctx") % 2, lax.axis_index("ctx") // a
    by_place = positions.reshape(b, nz, 2, n_tp * rows)
    key_pos = by_place.transpose(2, 0, 1, 3).reshape(2 * b, group_rows)
    own_pos = lax.dynamic_index_in_dim(key_pos, y * b + group, 0, keepdims=False)
    cos_tab, sin_tab = rope_tables(own_pos, HD)
    projected = jnp.einsum("td,kde->kte", rows_attn, qkv_w, preferred_element_type=f32)
    query_bf = rotate(projected[0], cos_tab, sin_tab, heads, HD).astype(bf16)
    query_bf = query_bf * jnp.asarray(score_scale, bf16)
    key_bf = rotate(projected[1], cos_tab, sin_tab, heads, HD).astype(bf16)
    value_bf = projected[2].astype(bf16)
    places = [(own_pos[:, None], VMEM), (key_pos.reshape(1, -1), VMEM)]
    n_keys = 2 * b * group_rows
    attn_bf, log_total, key_all, value_all, grad_rows, dn_w = comm_call(
        "attend", nz, 1, functools.partial(attend_work, heads),
        [(query_bf, VMEM), (over_groups(key_bf, 0), VMEM), (over_groups(value_bf, 0), VMEM)]
        + places + [(layer_output_gradient, VMEM)],
        [((group_rows, width), bf16, VMEM), ((group_rows, heads), f32, VMEM),
         ((n_keys, width), bf16, ANY), ((n_keys, width), bf16, ANY),
         ((group_rows, d_model), bf16, ANY)],
        [pltpu.VMEM((n_keys, width), bf16), pltpu.VMEM((n_keys, width), bf16)],
        [Swap(over_groups(down_weight, 1), 2, 1, units, depth, (units, d_model))],
    )
    dn_w = model_order(dn_w, 1)
    gu_all = over_groups(gate_up_weight, 1)
    partials = pltpu.VMEM((4 * nz, rows, d_model), bf16)
    hidden, rows_mlp, gate_w, up_w = comm_call(
        "middle", nz, 2, middle_work,
        [(attn_bf, VMEM), (out_w, VMEM), (block_input, VMEM), (gains, VMEM)],
        [((rows, d_model), f32, VMEM), ((group_rows, d_model), bf16, ANY)],
        [pltpu.VMEM((rows, d_model), bf16), partials] + scatter_bufs(nz, rows, d_model),
        [Swap(gu_all, 1, 2, units, depth, (d_model, units), p) for p in (0, 1)],
    )
    gate_w, up_w = model_order(gate_w, 0), model_order(up_w, 0)
    down_swap = Swap(None, 2, 1, units, depth, (nz * units, depth))
    residual_grad, branch_rows, gain_sum_2, mlp_part, gu_grad, dn_back = comm_call(
        "back", nz, 3, functools.partial(back_work, b),
        [(rows_mlp, ANY), (grad_rows, ANY), (gate_w, VMEM), (up_w, VMEM), (dn_w, VMEM),
         (hidden, VMEM), (layer_output_gradient, VMEM), (gains, VMEM)],
        [((rows, d_model), f32, VMEM), ((group_rows, d_model), bf16, ANY),
         ((1, d_model), f32, VMEM), ((4 * nz, rows, d_model), bf16, ANY),
         ((2, d_model, units), bf16, ANY)],
        [pltpu.VMEM((rows, d_model), f32), pltpu.VMEM((rows, d_model), bf16), partials, partials,
         pltpu.VMEM((3, group_rows, units), bf16),
         pltpu.VMEM((group_rows, d_model), bf16), pltpu.VMEM((group_rows, d_model), bf16),
         pltpu.VMEM((2, d_model, units), bf16), pltpu.VMEM((units, d_model), bf16),
         landing(nz, down_swap, (units, d_model))]
        + scatter_bufs(nz, rows, d_model),
        [down_swap],
        vmem=60,
    )
    out_weight_grad = jnp.einsum("te,td->ed", attn_bf, branch_rows, preferred_element_type=f32)
    attn_grad_bf = jnp.einsum("td,ed->te", branch_rows, out_w, preferred_element_type=f32).astype(bf16)
    gu_swap = Swap(gu_grad, 1, 2, units, depth, (2, depth, nz * units))
    query_grad, key_terms, value_terms, block_output, gu_back = comm_call(
        "attend_back", nz, 4, functools.partial(attend_back_work, heads),
        [(query_bf, VMEM), (key_all, VMEM), (value_all, VMEM)] + places
        + [(attn_bf, VMEM), (log_total, VMEM), (attn_grad_bf, VMEM), (mlp_part, VMEM),
           (hidden, VMEM)],
        [((group_rows, width), f32, VMEM), ((width, n_keys // 2), f32, VMEM),
         ((width, n_keys // 2), f32, VMEM), ((rows, d_model), bf16, VMEM)],
        [pltpu.VMEM((rows, d_model), f32), pltpu.VMEM((width, n_keys), f32),
         pltpu.VMEM((width, n_keys), f32), pltpu.VMEM((2, width, n_keys // 2), bf16),
         pltpu.VMEM((2, width, n_keys // 2), bf16), landing(nz, gu_swap, (2, d_model, units))]
        + scatter_bufs(nz, rows, d_model),
        [gu_swap],
        swap_spec=VMEM,
    )
    key_grad, value_grad = key_terms.T, value_terms.T
    if b > 1:
        key_grad = to_groups(key_grad.astype(bf16), 0).astype(f32)
        value_grad = to_groups(value_grad.astype(bf16), 0).astype(f32)
    query_raw = unrotate(query_grad, cos_tab, sin_tab, heads, HD).astype(bf16)
    key_raw = unrotate(key_grad, cos_tab, sin_tab, heads, HD).astype(bf16)
    value_raw = value_grad.astype(bf16)
    proj_grads = jnp.concatenate([query_raw, key_raw, value_raw], axis=1)
    qkv_grad = jnp.einsum(
        "td,kte->kde", rows_attn, jnp.stack([query_raw, key_raw, value_raw]),
        preferred_element_type=f32,
    )
    qkv_swap = Swap(
        swap_order(qkv_grad.astype(bf16), 1), 1, 2, width, depth, (3, depth, nz * width)
    )
    out_swap = Swap(
        swap_order(out_weight_grad.astype(bf16), 1), 2, 1, width, depth, (nz * width, depth)
    )
    layer_input_gradient, gain_sums, qkv_back, out_back = comm_call(
        "last", nz, 5, functools.partial(last_work, b),
        [(proj_grads, VMEM), (qkv_w, VMEM), (residual_grad, VMEM), (block_input, VMEM),
         (gains, VMEM), (gain_sum_2, VMEM)],
        [((rows, d_model), f32, VMEM), ((2, depth), f32, VMEM)],
        [pltpu.VMEM((rows, d_model), f32), pltpu.VMEM((2, d_model), f32),
         pltpu.VMEM((2, nz, 2, depth), f32), pltpu.VMEM((2 * nz + 3, 2, depth), f32),
         landing(nz, qkv_swap, (3, d_model, width)), landing(nz, out_swap, (width, d_model)),
         partials] + scatter_bufs(nz, rows, d_model),
        [qkv_swap, out_swap],
        swap_spec=VMEM,
    )
    if b > 1:
        gain_sums = lax.psum(gain_sums, "ctx", axis_index_groups=across)
    gain_cols = d_model // (n_ctx * n_tp)
    gain_part = lax.dynamic_slice_in_dim(
        gain_sums, (group * n_tp + lax.axis_index("tp")) * gain_cols, gain_cols, 1
    )
    return (
        block_output,
        layer_input_gradient,
        to_groups(qkv_back, 1).astype(f32),
        to_groups(out_back, 1).astype(f32),
        to_groups(gu_back, 1).astype(f32),
        to_groups(dn_back, 1).astype(f32),
        gain_part,
    )


def solution(mesh):
    placed = (
        P(("ctx", "tp"), None),
        P(None, "ctx", "tp"),
        P("tp", "ctx"),
        P(None, "ctx", "tp"),
        P("tp", "ctx"),
        P(None, "ctx"),
        P(),
        P(("ctx", "tp"), None),
    )
    return jax.shard_map(
        body,
        mesh=mesh,
        in_specs=placed,
        out_specs=(
            P(("ctx", "tp"), None),
            P(("ctx", "tp"), None),
            P(None, "ctx", "tp"),
            P("tp", "ctx"),
            P(None, "ctx", "tp"),
            P("tp", "ctx"),
            P(None, ("ctx", "tp")),
        ),
        check_vma=False,
    )
```

time: 1760 us -> 588 us (0.33)
  waiting for transfers between devices: 1530 us -> 0 us
  Pallas kernels: 0 us -> 529 us
  matrix products: 121 us -> 15.1 us
  blocking collectives: 22.6 us -> 0 us
  other arithmetic: 33.6 us -> 11.8 us
    reduce_scatter x9 -> x0, waiting for transfers between devices: 764 us -> none  [the longest x1 281 us: body(): lax.psum_scatter(gate_up_grad.astype(jnp.bfloat16), 'ctx', scatter_dimens...]
    all_gather x10 -> x0, waiting for transfers between devices: 630 us -> none  [the longest x1 229 us: body(): lax.all_gather(gate_up_weight, 'ctx', axis=1, tiled=True)]
    pallas_call x0 -> x6, Pallas kernels: none -> 529 us  [comm_call(): pl.pallas_call(functools.partial(comm_kernel, nz, work, swaps, len(ins),...]
    unnamed x21 -> x0, waiting for transfers between devices: 140 us -> none
    dot_general x18 -> x4, matrix products: 121 us -> 15.1 us  [the longest x1 6.01 us: body(): jnp.einsum('td,kte->kde', rows_attn, jnp.stack([query_raw, key_raw, value...]
    all_gather x1 -> x0, blocking collectives: 22.6 us -> none  [body(): lax.all_gather(norm_gains, 'ctx', axis=1, tiled=True)]
  transfers between devices with their start and end apart: 20 -> 0, of which waited for: 20 -> 0; matrix products, arithmetic and copies ran while one was open for 5% -> 0% of each run, Pallas kernels for 0% -> 0%
where the time goes in v1:
time: 588 us; the launch traced here: 583 us
  Pallas kernels  529 us (90%)
  local copies, waits for them, and re-layouts  25.7 us (4%)
  matrix products  15.1 us (3%)
  other arithmetic  11.8 us (2%)
    pallas_call x6, Pallas kernels, comm_call(): pl.pallas_call(functools.partial(comm_kernel, nz, work, swaps, len(ins),...  529 us
    unnamed x70, local copies, waits for them, and re-layouts  13.4 us

profile of v1, /device:TPU:0, one launch (start us, length us, event | category | flops | bytes accessed | tf_op | source)
XLA Modules:
  0.0 583.2 jit_solution(14944549877245604387)
XLA Ops:
  1.4 1.2 fusion.19
  3.8 1.1 copy-done.8
  6.6 78.9 %start.1 = (bf16[1024,2048]{1,0:T(8,128)(2,1)}, f32[2,2048]{1,0:T(2,128)S(1)}, bf16[3,2048,128]{2,1,0:T(8,128)(2,1)S(1)}, bf16[128,2048]{1,0:T(8,128)(2,1)S(1)}) custom-call(bf16[64,2048]{1,0:T(8,128)(2,1)S(1)} %copy-done, bf16[2,256]{1,0:T(2,128)(2,1)S(1)} %copy-done.28, bf16[3,256,512]{2,1,0:T(8,128)(2,1)S(1)} %copy-done.8, bf16[512,256]{1,0:T(8,128)(2,1)S(1)} %copy-done.24), custom_call_target="tpu_custom_call" | custom-call | tf_op jit(solution)/shard_map/start/pallas_call | solution.py:455
  85.5 4.7 fusion.10
  91.2 2.0 copy.25
  93.2 1.0 copy.24
  94.2 1.4 subtract_convert_fusion
  96.5 1.1 copy.28.refs_1_
  97.7 1.2 copy-done.7
  98.9 80.8 %attend.1 = (bf16[1024,128]{1,0:T(8,128)(2,1)S(1)}, f32[1024,2]{1,0:T(8,128)S(1)}, bf16[2048,128]{1,0:T(8,128)(2,1)S(1)}, bf16[2048,128]{1,0:T(8,128)(2,1)S(1)},...) custom-call(bf16[1024,128]{1,0:T(8,128)(2,1)S(1)} %copy.30.refs_0_, bf16[1024,128]{1,0:T(8,128)(2,1)S(1)} %copy.28.refs_1_, ...), custom_call_target="tpu_custom_call" | custom-call | tf_op jit(solution)/shard_map/attend/pallas_call | solution.py:455
  182.1 105.0 %middle.1 = (f32[64,2048]{1,0:T(8,128)S(1)}, bf16[1024,2048]{1,0:T(8,128)(2,1)}, bf16[2048,512]{1,0:T(8,128)(2,1)S(1)}, bf16[2048,512]{1,0:T(8,128)(2,1)S(1)}) custom-call(bf16[1024,128]{1,0:T(8,128)(2,1)S(1)} %get-tuple-element.40.refs_0_.refs_5_, bf16[128,2048]{1,0:T(8,128)(2,1)S(1)} %copy-done.11, bf16[64,2048]{1,0:T(8,128)(2,1)S(1)} %copy-done.1, ...), custom_call_target="tpu_custom_call" | custom-call | tf_op jit(solution)/shard_map/middle/pallas_call | solution.py:455
  287.9 1.3 copy-done.4
  289.3 1.3 copy-done.5
  290.6 101.2 %back.1 = (f32[64,2048]{1,0:T(8,128)}, bf16[1024,2048]{1,0:T(8,128)(2,1)}, f32[1,2048]{1,0:T(1,128)}, bf16[16,64,2048]{2,1,0:T(8,128)(2,1)}, bf16[2,2048,512]{2,1,0:T(8,128)(2,1)}, /*index=5*/bf16[2048,256]{1,0:T(8,128)(2,1)}) custom-call(bf16[1024,2048]{1,0:T(8,128)(2,1)} %get-tuple-element.44.refs_0_, bf16[1024,2048]{1,0:T(8,128)(2,1)} %get-tuple-element.45.refs_1_, ...), custom_call_target="tpu_custom_call" | custom-call | tf_op jit(solution)/shard_map/back/pallas_call | solution.py:455
  391.8 3.6 convolution_convert_fusion.1.refs_7_
  395.4 99.1 %attend_back.1 = (f32[1024,128]{1,0:T(8,128)S(1)}, f32[128,1024]{1,0:T(8,128)S(1)}, f32[128,1024]{1,0:T(8,128)S(1)}, bf16[64,2048]{1,0:T(8,128)(2,1)S(1)}, bf16[2,256,2048]{2,1,0:T(8,128)(2,1)}) custom-call(bf16[1024,128]{1,0:T(8,128)(2,1)S(1)} %copy.30.refs_0_, bf16[2048,128]{1,0:T(8,128)(2,1)S(1)} %copy-done.16, bf16[2048,128]{1,0:T(8,128)(2,1)S(1)} %copy-done.18, ...), custom_call_target="tpu_custom_call" | custom-call | tf_op jit(solution)/shard_map/attend_back/pallas_call | solution.py:455
  496.4 1.2 copy.32
  497.7 1.1 multiply_subtract_fusion.1
  501.3 1.2 pad_maximum_fusion.refs_0_
  503.4 6.0 %fusion.7.refs_6_ = bf16[3,2048,128]{2,1,0:T(8,128)(2,1)} fusion(bf16[1024,2048]{1,0:T(8,128)(2,1)} %get-tuple-element.37, bf16[1,1024,128]{2,1,0:T(8,128)(2,1)} %bitcast.58, bf16[1,1024,128]{2,1,0:T(8,128)(2,1)} %copy.37, bf16[1,1024,128]{2,1,0:T(8,128)(2,1)} %copy.36), kind=kOutput, calls=%fused_computation.5 | convolution fusion | flops 1612185600 | bytes 6553600 | tf_op jit(solution)/shard_map/td,kte->kde/dot_general | solution.py:964
  509.4 64.1 %last.1 = (f32[64,2048]{1,0:T(8,128)S(1)}, f32[2,256]{1,0:T(2,128)S(1)}, bf16[3,256,512]{2,1,0:T(8,128)(2,1)S(1)}, bf16[512,256]{1,0:T(8,128)(2,1)S(1)}) custom-call(bf16[1024,384]{1,0:T(8,128)(2,1)S(1)} %pad_maximum_fusion.refs_0_, bf16[3,2048,128]{2,1,0:T(8,128)(2,1)S(1)} %get-tuple-element.36.refs_1_, f32[64,2048]{1,0:T(8,128)S(1)} %copy-done.9, ...), custom_call_target="tpu_custom_call" | custom-call | tf_op jit(solution)/shard_map/last/pallas_call | solution.py:455
  575.0 1.4 convert_element_type.95
  576.4 1.5 convert_element_type.98
  578.8 2.5 convert_element_type.97
  (86 shorter events, 17.7 us)
Async XLA Ops:
  2.6 91.6 %copy-start.31 = (f32[1024,32]{0,1:T(8,128)}, f32[1024,32]{0,1:T(8,128)S(1)}, u32[]{:S(2)}) copy-start(f32[1024,32]{0,1:T(8,128)S(1)} %get-tuple-element.83) | copy-start | bytes 393220
  3.8 1.1 copy-start.8
  85.5 4.7 copy-start.10
  85.5 96.6 %copy-start.25 = (f32[2,2048]{1,0:T(2,128)}, f32[2,2048]{1,0:T(2,128)S(1)}, u32[]{:S(2)}) copy-start(f32[2,2048]{1,0:T(2,128)S(1)} %get-tuple-element.43.refs_3_.refs_7_.refs_4_) | copy-start | bytes 49156
  94.2 3.4 copy-start.6
  96.3 85.8 %copy-start.1 = (bf16[64,2048]{1,0:T(8,128)(2,1)S(1)}, bf16[64,2048]{1,0:T(8,128)(2,1)}, u32[]{:S(2)}) copy-start(bf16[64,2048]{1,0:T(8,128)(2,1)} %refs_3_.3) | copy-start | bytes 786436
  97.7 1.2 copy-start.7
  98.9 83.2 %copy-start.11 = (bf16[128,2048]{1,0:T(8,128)(2,1)S(1)}, bf16[128,2048]{1,0:T(8,128)(2,1)}, u32[]{:S(2)}) copy-start(bf16[128,2048]{1,0:T(8,128)(2,1)} %copy-done.10) | copy-start | bytes 1572868
  287.9 1.3 copy-start.4
  289.3 1.3 copy-start.5
  290.6 101.2 %copy-start.12 = (bf16[128,2048]{1,0:T(8,128)(2,1)S(1)}, bf16[128,2048]{1,0:T(8,128)(2,1)}, u32[]{:S(2)}) copy-start(bf16[128,2048]{1,0:T(8,128)(2,1)} %copy-done.10) | copy-start | bytes 1572868
  391.8 3.6 copy-start.3
  391.8 3.6 copy-start.14
  391.8 3.6 copy-start.16
  391.8 3.6 copy-start.18
  395.4 99.1 %copy-start.29 = (bf16[1024,2048]{1,0:T(8,128)(2,1)S(1)}, bf16[1024,2048]{1,0:T(8,128)(2,1)}, u32[]{:S(2)}) copy-start(bf16[1024,2048]{1,0:T(8,128)(2,1)} %get-tuple-element.50) | copy-start | bytes 12582916
  494.6 3.1 copy-start.32
  495.6 2.1 copy-start.20
  503.4 6.0 %copy-start.9 = (f32[64,2048]{1,0:T(8,128)S(1)}, f32[64,2048]{1,0:T(8,128)}, u32[]{:S(2)}) copy-start(f32[64,2048]{1,0:T(8,128)} %get-tuple-element.57.refs_2_) | copy-start | bytes 1572868
  503.4 6.0 %copy-start.26 = (f32[2,2048]{1,0:T(2,128)S(1)}, f32[2,2048]{1,0:T(2,128)}, u32[]{:S(2)}) copy-start(f32[2,2048]{1,0:T(2,128)} %copy-done.25) | copy-start | bytes 49156
  503.4 6.0 %copy-start.27 = (f32[1,2048]{1,0:T(1,128)S(1)}, f32[1,2048]{1,0:T(1,128)}, u32[]{:S(2)}) copy-start(f32[1,2048]{1,0:T(1,128)} %get-tuple-element.58.refs_5_) | copy-start | bytes 24580
  573.6 2.8 copy-start.33
  576.4 2.3 copy-start.30
  578.8 2.5 copy-start.23
  (10 other events, 8.6 us)

commit v2 on v1

--- a/solution.py
+++ b/solution.py
@@ -57,13 +57,18 @@
     def device(self, z, y, x, k):
         return {"ctx": self.first + 2 * z + y, "tp": 2 * x + k}
 
+    def elsewhere(self, g, flip):
+        n = lax.axis_size("ctx")
+        y = self.y + flip * (1 - 2 * self.y)
+        return {"ctx": (self.first + g * 2 * self.nz) % n + 2 * self.z + y}
+
 
 def slot_of(z, x, k):
     return (z * 2 + x) * 2 + k
 
 
 class Comm:
-    def __init__(self, at, pool):
+    def __init__(self, at, pool, groups=1):
         self.at, self.pool, self.used, self.ends, self.late = at, pool, 0, [], []
         z, y, x, k, nz = at.z, at.y, at.x, at.k, at.nz
         self.to_x = at.device(z, y, 1 - x, k)
@@ -71,6 +76,8 @@
         self.to_y = at.device(z, 1 - y, x, k)
         self.to_xk = at.device(z, y, 1 - x, 1 - k)
         peers = [self.to_x, self.to_k, self.to_y, self.to_xk]
+        self.afar = [(g, f, at.elsewhere(g, f)) for g in range(1, groups) for f in (0, 1)]
+        peers += [device for _, _, device in self.afar]
         peers += [at.device((z + d) % nz, y, x, k) for d in range(1, nz)]
         barrier = pltpu.get_barrier_semaphore()
         for peer in peers:
@@ -117,10 +124,13 @@
         if copies:
             self.ends.append((cond, end))
 
-    def keep(self, src, dst):
+    def move(self, src, dst):
         copy = pltpu.make_async_copy(src, dst, self.sem())
         copy.start()
-        self.ends.append((None, copy.wait))
+        return copy.wait
+
+    def keep(self, src, dst):
+        self.ends.append((None, self.move(src, dst)))
 
     def arrive(self, buf, recv_sem):
         pltpu.make_async_remote_copy(
@@ -206,7 +216,7 @@
             cond,
         )
         if d == 0:
-            comm.keep(here, part(slot))
+            moved = comm.move(here, part(slot))
         yield
     for i, (d, side, zi, cond) in enumerate(places):
         slot = slot_of(zi, 1 - x, k)
@@ -217,6 +227,7 @@
     for h, xh in enumerate((x, 1 - x)):
         for i, (d, side, zi, cond) in enumerate(places):
             comm.step([(part(slot_of(zi, xh, 1 - k)), sem_k[h * n + i])], [], cond)
+    moved()
 
 
 def add_rows(dst, terms):
@@ -343,9 +354,10 @@
 
 
 class Swap:
-    def __init__(self, array, unit_axis, feature_axis, units, depth, shape, plane=None):
+    def __init__(self, array, unit_axis, feature_axis, units, depth, shape, plane=None, groups=1):
         self.array, self.shape, self.plane = array, shape, plane
         self.unit_axis, self.feature_axis, self.units, self.depth = unit_axis, feature_axis, units, depth
+        self.groups = groups if feature_axis == 2 else 1
         self.out = jax.ShapeDtypeStruct(shape, bf16)
 
     def of_units(self, ref, z):
@@ -356,37 +368,53 @@
     def of_features(self, ref, z, y):
         return along(ref, self.feature_axis, 2 * z + y, self.depth)
 
-
-def swap_in(comm, swaps, srcs, dsts):
+    def runs(self, ref, nz, z, y):
+        if self.groups == 1:
+            return [self.of_features(ref, z, y)]
+        r = self.depth // self.groups
+        return [along(ref, 2, i * 2 * nz + 2 * z + y, r) for i in range(self.groups)]
+
+    def cuts(self, piece):
+        if self.groups == 1:
+            return [piece]
+        r = self.depth // self.groups
+        return [along(piece, 2, i, r) for i in range(self.groups)]
+
+
+def swap_in(comm, one, src, dst):
     at = comm.at
     z, y, x, k, nz = at.z, at.y, at.x, at.k, at.nz
-    sem_z = [comm.sems(nz) for _ in swaps]
-    sem_y = [comm.sems(nz) for _ in swaps]
+    sem_z = [comm.sems(one.groups) for _ in range(nz)]
+    sem_y = [comm.sems(one.groups) for _ in range(nz)]
+    moved = []
 
     def sends():
-        for i, one in enumerate(swaps):
-            mine = one.of_features(dsts[i], z, y)
-            for d in range(1, nz):
-                zi = (z + d) % nz
-                comm.step([], [(one.of_units(srcs[i], zi), mine, sem_z[i][d], at.device(zi, y, x, k))])
-                yield
-            own = one.of_units(srcs[i], z)
-            comm.step([], [(own, mine, sem_y[i][0], comm.to_y)])
-            comm.keep(own, mine)
+        mine = one.runs(dst, nz, z, y)
+        for d in range(1, nz):
+            zi = (z + d) % nz
+            parts = one.cuts(one.of_units(src, zi))
+            for part, to, sem in zip(parts, mine, sem_z[d]):
+                comm.step([], [(part, to, sem, at.device(zi, y, x, k))])
             yield
+        for part, to, sem in zip(one.cuts(one.of_units(src, z)), mine, sem_y[0]):
+            comm.step([], [(part, to, sem, comm.to_y)])
+            moved.append(comm.move(part, to))
+        yield
 
     def passes():
-        for i, one in enumerate(swaps):
-            for d in range(1, nz):
-                come = one.of_features(dsts[i], (z + nz - d) % nz, y)
-                comm.step([(come, sem_z[i][d])], [(come, come, sem_y[i][d], comm.to_y)])
-                yield
-        for i, one in enumerate(swaps):
-            for d in range(nz):
-                zi = (z + nz - d) % nz
-                comm.late.append((one.of_features(dsts[i], zi, 1 - y), sem_y[i][d]))
-
-    return sends(), passes()
+        for d in range(1, nz):
+            for run, sem, on in zip(one.runs(dst, nz, (z + nz - d) % nz, y), sem_z[d], sem_y[d]):
+                comm.step([(run, sem)], [(run, run, on, comm.to_y)])
+            yield
+
+    def arrivals():
+        for d in range(nz):
+            for run, sem in zip(one.runs(dst, nz, (z + nz - d) % nz, 1 - y), sem_y[d]):
+                comm.arrive(run, sem)
+        for wait in moved:
+            wait()
+
+    return sends(), passes(), arrivals
 
 
 def add_piece(dst, src):
@@ -397,39 +425,53 @@
         add_rows(dst, [dst, src])
 
 
-def swap_out(comm, swaps, srcs, dsts, landed):
+def swap_out_y(comm, one, src, landed):
+    at = comm.at
+    z, y, nz = at.z, at.y, at.nz
+    order = list(range(1, nz)) + [0]
+    sems = comm.sems(nz)
+
+    def sends():
+        for d in order:
+            zi = (z + d) % nz
+            comm.step([], [(one.of_features(src, zi, 1 - y), landed.at[zi], sems[d], comm.to_y)])
+            yield
+
+    def sums():
+        for d in order:
+            zi = (z + d) % nz
+            comm.arrive(landed.at[zi], sems[d])
+            add_piece(landed.at[zi], one.of_features(src, zi, y))
+            yield
+
+    return sends(), sums()
+
+
+def swap_out_z(comm, one, summed, dst):
     at = comm.at
     z, y, x, k, nz = at.z, at.y, at.x, at.k, at.nz
-    sem_y = [comm.sems(nz) for _ in swaps]
-    sem_z = [comm.sems(nz) for _ in swaps]
-
-    def sends():
-        for i, one in enumerate(swaps):
-            for d in list(range(1, nz)) + [0]:
-                zi = (z + d) % nz
-                comm.step(
-                    [], [(one.of_features(srcs[i], zi, 1 - y), landed[i].at[zi], sem_y[i][d], comm.to_y)]
-                )
-                yield
-
-    def passes():
-        for i, one in enumerate(swaps):
-            mine = one.of_units(dsts[i], z)
-            for d in list(range(1, nz)) + [0]:
-                zi = (z + d) % nz
-                buf = landed[i].at[zi]
-                comm.arrive(buf, sem_y[i][d])
-                add_piece(buf, one.of_features(srcs[i], zi, y))
-                if d:
-                    comm.step([], [(buf, mine, sem_z[i][d], at.device(zi, y, x, k))])
-                else:
-                    comm.keep(buf, mine)
-                yield
-        for i, one in enumerate(swaps):
-            for d in range(1, nz):
-                comm.late.append((one.of_units(dsts[i], (z + nz - d) % nz), sem_z[i][d]))
-
-    return sends(), passes()
+    mine = one.of_units(dst, z)
+    sems = comm.sems(nz)
+    for d in list(range(1, nz)) + [0]:
+        zi = (z + d) % nz
+        if d:
+            comm.step([], [(summed.at[zi], mine, sems[d], at.device(zi, y, x, k))])
+            comm.late.append((one.of_units(dst, (z + nz - d) % nz), sems[d]))
+        else:
+            comm.keep(summed.at[zi], mine)
+        yield
+
+
+def paired(first, second):
+    for _ in first:
+        next(second, None)
+        yield
+    yield from second
+
+
+def chain(*many):
+    for steps in many:
+        yield from steps
 
 
 def landing(nz, one, user_shape):
@@ -438,26 +480,26 @@
     return pltpu.VMEM((nz, *shape), bf16)
 
 
-def comm_kernel(nz, work, swaps, n_in, n_out, *refs):
+def comm_kernel(nz, groups, work, swaps, extra, n_in, n_out, *refs):
     given = [one for one in swaps if one.array is not None]
     m, g = len(swaps), len(given)
     ins, srcs = refs[:n_in], refs[n_in : n_in + g]
     outs = refs[n_in + g : n_in + g + n_out]
     dsts = refs[n_in + g + n_out : n_in + g + n_out + m]
     scratch = refs[n_in + g + n_out + m :]
-    comm = Comm(Place(nz), scratch[-1])
-    work(comm, (swaps, srcs, dsts), ins, outs, scratch[:-1])
+    comm = Comm(Place(nz), scratch[-1], groups)
+    work(comm, (swaps + extra, srcs, dsts), ins, outs, scratch[:-1])
     comm.finish()
 
 
-def comm_call(name, nz, collective, work, ins, outs, scratch, swaps, swap_spec=ANY, vmem=48):
+def comm_call(name, nz, collective, work, ins, outs, scratch, swaps, swap_spec=ANY, vmem=48, groups=1, extra=()):
     given = [one.array for one in swaps if one.array is not None]
     return pl.pallas_call(
-        functools.partial(comm_kernel, nz, work, swaps, len(ins), len(outs)),
+        functools.partial(comm_kernel, nz, groups, work, swaps, list(extra), len(ins), len(outs)),
         out_shape=[jax.ShapeDtypeStruct(s, d) for s, d, _ in outs] + [one.out for one in swaps],
         in_specs=[s for _, s in ins] + [swap_spec] * len(given),
         out_specs=[s for _, _, s in outs] + [ANY] * len(swaps),
-        scratch_shapes=scratch + [DMA((600,))],
+        scratch_shapes=scratch + [DMA((700,))],
         compiler_params=pltpu.CompilerParams(
             collective_id=collective, has_side_effects=True, vmem_limit_bytes=vmem * 2**20
         ),
@@ -525,27 +567,6 @@
         gains[:, col : col + r] = landed[c % 2, c // 2, :, lo : lo + r].astype(f32)
 
 
-def start_work(groups, comm, swap, ins, outs, scratch):
-    x_ref, gain_ref = ins
-    rows_attn, gains = outs
-    normed, landed = scratch
-    at = comm.at
-    gains_of_group(comm, groups, gain_ref, landed, gains)
-
-    def norm(r):
-        x = x_ref[r, :].astype(f32)
-        normed[r, :] = (x * inv_rms(x) * gains[0:1, :]).astype(bf16)
-
-    rows = x_ref.shape[0]
-    by_rows(0, rows, norm)
-    shards = gather_steps(comm, normed, rows_attn, 0, rows)
-    sends, passes = swap_in(comm, *swap)
-    advance(shards, 1)
-    advance(sends, at.nz)
-    take_turns(shards, sends)
-    exhaust(passes)
-
-
 def product_into(p_ref, rows, at_slot, lhs, rhs, rhs_dims):
     n = p_ref.shape[2]
     wide = math.gcd(n, 512)
@@ -620,56 +641,123 @@
     yield from row_blocks(q_ref.shape[0], k_ref.shape[0], block)
 
 
-def attend_work(heads, comm, swap, ins, outs, scratch):
-    q_ref, k_ref, v_ref, at_q, at_k, dy_ref = ins
-    o_ref, lse_ref, k_out, v_out, grad_rows = outs
-    k_all, v_all = scratch
+def forward_work(heads, groups, comm, swap, ins, outs, scratch):
+    x_ref, gain_ref, cos, sin, at_q, at_k = ins
+    gains, q_ref, o_ref, lse_ref, hidden, rows_attn, k_out, v_out, rows_mlp = outs
+    normed, landed, rows_v, qkv_v, out_v, k_all, v_all, p_ref = scratch[:8]
+    bufs = scratch[8:]
+    swaps, srcs, dsts = swap
     at = comm.at
-    y, keys = at.y, k_ref.shape[0]
-
-    def half(ref, yy):
-        return ref.at[pl.ds(pl.multiple_of(yy * keys, keys), keys), :]
-
-    sem = comm.sems(2)
-    for i, (mine, both) in enumerate(((k_ref, k_all), (v_ref, v_all))):
-        comm.step([], [(mine, half(both, y), sem[i], comm.to_y)])
-        half(both, y)[...] = mine[...]
-    grads = gather_steps(comm, dy_ref, grad_rows, 0, dy_ref.shape[0])
-    sends, passes = swap_in(comm, *swap)
-    advance(grads, 1)
-    advance(sends, 4)
-    advance(grads, 2)
-    for i, (both, out) in enumerate(((k_all, k_out), (v_all, v_out))):
-        comm.arrive(half(both, 1 - y), sem[i])
-        comm.keep(both, out)
-    compute = attend(heads, q_ref, k_all, v_all, at_q, at_k, o_ref, lse_ref)
-    take_turns(grads, sends, compute)
-    exhaust(passes)
+    y, nz = at.y, at.nz
+    rows, d_model = x_ref.shape
+    tall = 4 * rows
+    keys = q_ref.shape[0]
+    width = q_ref.shape[1]
+
+    places = (qkv_v, out_v) + tuple(dsts[2:])
+    qkv, out, down, gate, up = [swap_in(comm, *v) for v in zip(swaps, srcs, places)]
+    exhaust(qkv[0])
+    gains_of_group(comm, groups, gain_ref, landed, gains)
+
+    def norm_1(r):
+        x = x_ref[r, :].astype(f32)
+        normed[r, :] = (x * inv_rms(x) * gains[0:1, :]).astype(bf16)
+
+    by_rows(0, rows, norm_1)
+    shards = gather_steps(comm, normed, rows_v, 0, rows)
+    advance(shards, z_steps(at))
+    take_turns(shards, chain(out[0], qkv[1]))
+    exhaust(down[0])
+    qkv[2]()
+    comm.keep(qkv_v, dsts[0])
+    comm.keep(rows_v, rows_attn)
+
+    def half(ref, g, yy):
+        return ref.at[pl.ds(pl.multiple_of((yy * groups + g) * keys, keys), keys), :]
+
+    group = at.first // (2 * nz)
+    mine = [half(ref, group, y) for ref in (k_all, v_all)]
+    low = lax.broadcasted_iota(jnp.int32, (1, width), 1) % HD < HD // 2
+
+    def project(i, _):
+        r = pl.ds(pl.multiple_of(i * tall, tall), tall)
+        block = rows_v[r, :]
+
+        def turned(p):
+            u = jnp.dot(block, qkv_v[p], preferred_element_type=f32)
+            other = jnp.where(
+                low, pltpu.roll(u, width - HD // 2, 1), pltpu.roll(u, HD // 2, 1)
+            )
+            return (u * cos[r, :] + other * sin[r, :]).astype(bf16)
+
+        q_ref[r, :] = turned(0) * jnp.asarray(HD ** (-0.5), bf16)
+        mine[0][r, :] = turned(1)
+        mine[1][r, :] = jnp.dot(block, qkv_v[2], preferred_element_type=f32).astype(bf16)
+        return 0
+
+    lax.fori_loop(0, nz, project, 0)
+    sem = comm.sems(4 * groups)
+    for i, ref in enumerate(mine):
+        comm.step([], [(ref, ref, sem[i], comm.to_y)])
+        for g, f, device in comm.afar:
+            comm.step([], [(ref, ref, sem[2 + (2 * g + f) * 2 + i - 2], device)])
+    exhaust(gate[0])
+    exhaust(out[1])
+    out[2]()
+    comm.keep(out_v, dsts[1])
+    for i, (ref, dst) in enumerate(((k_all, k_out), (v_all, v_out))):
+        comm.arrive(half(ref, group, 1 - y), sem[i])
+        for g, f, device in comm.afar:
+            come = half(ref, (group + groups - g) % groups, y + f * (1 - 2 * y))
+            comm.arrive(come, sem[2 + (2 * g + f) * 2 + i - 2])
+        comm.keep(ref, dst)
+    take_turns(
+        attend(heads, q_ref, k_all, v_all, at_q, at_k, o_ref, lse_ref), chain(down[1], gate[1])
+    )
+
+    def norm_2(r):
+        h = hidden[r, :] + x_ref[r, :].astype(f32)
+        hidden[r, :] = h
+        normed_2[r, :] = (h * inv_rms(h) * gains[1:2, :]).astype(bf16)
+
+    def produce(zi):
+        r = pl.ds(pl.multiple_of(zi * tall, tall), tall)
+        product_into(p_ref, rows, zi * 4, [o_ref[r, :]], [out_v], [0])
+
+    normed_2, total = bufs[3], bufs[4]
+    steps = Scatter(comm, p_ref, bufs[:3], total).steps(produce)
+    advance(up[0], 1)
+    exhaust(steps)
+    for c, lo, col, r in feature_pieces(nz, groups, d_model) if groups > 1 else [(0, 0, 0, d_model)]:
+        frm = c * (d_model // (2 * nz)) + lo
+        hidden[:, col : col + r] = total[:, frm : frm + r]
+    by_rows(0, rows, norm_2)
+    shards = gather_steps(comm, normed_2, rows_mlp, 0, rows)
+    advance(shards, z_steps(at))
+    take_turns(shards, up[0])
+    exhaust(up[1])
+    for one in (down, gate, up):
+        one[2]()
 
 
 def attend_back_work(heads, comm, swap, ins, outs, scratch):
-    q_ref, k_ref, v_ref, at_q, at_k, o_ref, lse_ref, do_ref, p_ref, hidden = ins
-    dq_ref, dk_out, dv_out, block_out = outs
-    total, dk_ref, dv_ref, going, come, gu_landed = scratch[:6]
-    bufs = scratch[6:]
+    q_ref, k_ref, v_ref, at_q, at_k, o_ref, lse_ref, do_ref, gate_sum, up_grad = ins
+    dq_ref, dk_out, dv_out = outs
+    dk_ref, dv_ref, going, come, up_landed = scratch
+    (gate, up), _, dsts = swap
     at = comm.at
     y, keys = at.y, k_ref.shape[0] // 2
 
     def half(ref, yy):
         return ref.at[:, pl.ds(pl.multiple_of(yy * keys, keys), keys)]
 
-    def out(r):
-        block_out[r, :] = (hidden[r, :] + total[r, :]).astype(bf16)
-
-    sends, passes = swap_out(comm, *swap, [gu_landed])
+    sends, sums = swap_out_y(comm, up, up_grad, up_landed)
     exhaust(sends)
-    steps = Scatter(comm, p_ref, bufs, total).steps()
+    exhaust(swap_out_z(comm, gate, gate_sum, dsts[0]))
     compute = attend_back(
         heads, q_ref, k_ref, v_ref, at_q, at_k, o_ref, lse_ref, do_ref, dq_ref, dk_ref, dv_ref
     )
-    advance(steps, 2)
-    take_turns(compute, steps, passes)
-    by_rows(0, hidden.shape[0], out)
+    take_turns(compute, paired(sums, swap_out_z(comm, up, up_landed, dsts[1])))
     sem = comm.sems(2)
     for i, ref in enumerate((dk_ref, dv_ref)):
         going[i] = half(ref, 1 - y)[...].astype(bf16)
@@ -679,79 +767,57 @@
         dst[...] = half(ref, y)[...] + come[i].astype(f32)
 
 
-def middle_work(comm, swap, ins, outs, scratch):
-    attn, out_w, x_ref, gains = ins
-    hidden, rows_mlp = outs
-    normed, p_ref, bufs = scratch[0], scratch[1], scratch[2:]
-    rows = x_ref.shape[0]
-
-    def norm(r):
-        h = hidden[r, :] + x_ref[r, :].astype(f32)
-        hidden[r, :] = h
-        normed[r, :] = (h * inv_rms(h) * gains[1:2, :]).astype(bf16)
-
-    def produce(zi):
-        r = pl.ds(pl.multiple_of(zi * 4 * rows, 4 * rows), 4 * rows)
-        product_into(p_ref, rows, zi * 4, [attn[r, :]], [out_w], [0])
-
-    sends, passes = swap_in(comm, *swap)
-    advance(sends, comm.at.nz)
-    steps = Scatter(comm, p_ref, bufs, hidden).steps(produce)
-    exhaust(steps)
-    by_rows(0, rows, norm)
-    shards = gather_steps(comm, normed, rows_mlp, 0, rows)
-    advance(shards, z_steps(comm.at))
-    take_turns(shards, sends, passes)
-
-
 def norm_back(grad, unit, rms, gain):
     unit_grad = grad * gain
     return rms * (unit_grad - unit * jnp.mean(unit_grad * unit, axis=-1, keepdims=True))
 
 
 def back_work(groups, comm, swap, ins, outs, scratch):
-    rows_mlp, grad_rows, gate_w, up_w, dn_w, hidden, dy_ref, gains = ins
-    residual, branch_rows, gain_sum, q_out, gu_out = outs
-    total, rounded, p_ref, q_ref, gates, n2, dy, gu_g, dn_g, dn_landed = scratch[:10]
-    bufs = scratch[10:]
+    rows_mlp, gate_w, up_w, dn_w, hidden, dy_ref, gains = ins
+    residual, branch_rows, gain_sum, block_out, gate_out, up_out = outs
+    total, rounded, p_ref, q_ref, pre, gates, n2, dy, gate_g, up_g, dn_g, dn_landed, gate_landed = scratch[:13]
+    bufs, bufs_q = scratch[13:16], scratch[16:19]
+    (down, gate_swap), _, dsts = swap
     at = comm.at
     nz = at.nz
     rows = hidden.shape[0]
     tall = 4 * rows
     gain_sum[...] = jnp.zeros_like(gain_sum)
-    sems = comm.sems(2 * nz)
+    sems = comm.sems(nz)
 
     def load(t, zi):
         r = pl.ds(pl.multiple_of(zi * tall, tall), tall)
-        return [
-            pltpu.make_async_copy(rows_mlp.at[r, :], n2.at[r, :], sems[2 * t]),
-            pltpu.make_async_copy(grad_rows.at[r, :], dy.at[r, :], sems[2 * t + 1]),
-        ]
+        return pltpu.make_async_copy(rows_mlp.at[r, :], n2.at[r, :], sems[t])
 
     main = Scatter(comm, p_ref, bufs, total)
     for t in range(nz):
-        for copy in load(t, main.targets[t][2]):
-            copy.start()
+        load(t, main.targets[t][2]).start()
     turn = iter(range(nz))
 
-    def produce(zi):
-        for copy in load(next(turn), zi):
-            copy.wait()
+    def forward(zi):
+        load(next(turn), zi).wait()
         r = pl.ds(pl.multiple_of(zi * tall, tall), tall)
-        x, g = n2[r, :], dy[r, :]
+        x = n2[r, :]
         gate = jnp.dot(x, gate_w[...], preferred_element_type=f32)
         up = jnp.dot(x, up_w[...], preferred_element_type=f32)
-        grad = lax.dot_general(g, dn_w[...], (((1,), (1,)), ((), ())), preferred_element_type=f32)
+        pre[0, r, :] = gate
+        pre[1, r, :] = up
+        hid = (gate * jax.nn.sigmoid(gate) * up).astype(bf16)
+        gates[2, r, :] = hid
+        product_into(q_ref, rows, zi * 4, [hid], [dn_w], [0])
+
+    def backward(zi):
+        r = pl.ds(pl.multiple_of(zi * tall, tall), tall)
+        grad = lax.dot_general(
+            dy[r, :], dn_w[...], (((1,), (1,)), ((), ())), preferred_element_type=f32
+        )
+        gate, up = pre[0, r, :], pre[1, r, :]
         sig = jax.nn.sigmoid(gate)
-        act = gate * sig
-        hid = (act * up).astype(bf16)
         gate_grad = (grad * up * (sig * (1.0 + gate * (1.0 - sig)))).astype(bf16)
-        up_grad = (grad * act).astype(bf16)
+        up_grad = (grad * (gate * sig)).astype(bf16)
         gates[0, r, :] = gate_grad
         gates[1, r, :] = up_grad
-        gates[2, r, :] = hid
         product_into(p_ref, rows, zi * 4, [gate_grad, up_grad], [gate_w, up_w], [1, 1])
-        product_into(q_ref, rows, zi * 4, [hid], [dn_w], [0])
 
     def back(r):
         h = hidden[r, :]
@@ -762,37 +828,51 @@
         residual[r, :] = dh
         rounded[r, :] = dh.astype(bf16)
 
-    def gradients():
+    def out(r):
+        block_out[r, :] = (hidden[r, :] + residual[r, :]).astype(bf16)
+
+    def gradients(which):
         d_model = n2.shape[1]
         depth = d_model // (2 * nz)
         over_rows = (((0,), (0,)), ((), ()))
         pieces = feature_pieces(nz, groups, d_model)
-        per = max(1, len(pieces) // 8)
+        per = max(1, len(pieces) // 4)
         for j in range(0, len(pieces), per):
             for c, lo, col, r in pieces[j : j + per]:
                 f, to = slice(col, col + r), slice(c * depth + lo, c * depth + lo + r)
-                for p in (0, 1):
-                    gu_g[p, to, :] = lax.dot_general(
-                        n2[:, f], gates[p], over_rows, preferred_element_type=f32
+                if which == 2:
+                    dn_g[:, to] = lax.dot_general(
+                        gates[2], dy[:, f], over_rows, preferred_element_type=f32
                     ).astype(bf16)
-                dn_g[:, to] = lax.dot_general(
-                    gates[2], dy[:, f], over_rows, preferred_element_type=f32
-                ).astype(bf16)
+                else:
+                    (gate_g, up_g)[which][to, :] = lax.dot_general(
+                        n2[:, f], gates[which], over_rows, preferred_element_type=f32
+                    ).astype(bf16)
             yield
 
-    steps = main.steps(produce)
-    others = gradients()
-    advance(steps, 3 * nz - 2)
-    comm.keep(q_ref, q_out)
-    take_turns(steps, others)
-    comm.keep(gu_g, gu_out)
+    shards = gather_steps(comm, dy_ref, dy, 0, rows)
+    side = Scatter(comm, q_ref, bufs_q, residual).steps(forward)
+    advance(shards, 1)
+    for _ in range(3 * nz - 3):
+        next(side)
+        advance(shards, 1)
+    take_turns(shards, side)
+    by_rows(0, rows, out)
+    steps = main.steps(backward)
+    down_sends, down_sums = swap_out_y(comm, down, dn_g, dn_landed)
+    gate_sends, gate_sums = swap_out_y(comm, gate_swap, gate_g, gate_landed)
+    advance(steps, 3 * nz - 3)
+    take_turns(
+        steps,
+        chain(gradients(2), down_sends, gradients(0), gate_sends, gradients(1)),
+    )
+    comm.keep(up_g, up_out)
     by_rows(0, rows, back)
     shards = gather_steps(comm, rounded, branch_rows, 0, rows)
-    sends, passes = swap_out(comm, swap[0], (dn_g,), swap[2], [dn_landed])
-    advance(shards, 1)
-    exhaust(sends)
-    advance(shards, z_steps(at) - 1)
-    take_turns(shards, passes)
+    advance(shards, z_steps(at))
+    take_turns(shards, paired(down_sums, swap_out_z(comm, down, dn_landed, dsts[0])))
+    exhaust(gate_sums)
+    comm.keep(gate_landed, gate_out)
 
 
 def last_work(groups, comm, swap, ins, outs, scratch):
@@ -818,9 +898,17 @@
         lhs = [proj_grads[r, p * width : (p + 1) * width] for p in range(3)]
         product_into(p_ref, rows, zi * 4, lhs, [qkv_w.at[p] for p in range(3)], [1] * 3)
 
-    sends, passes = swap_out(comm, *swap, [qkv_landed, out_landed])
-    exhaust(sends)
-    take_turns(Scatter(comm, p_ref, bufs, total).steps(produce), passes)
+    (qkv, out), srcs, dsts = swap
+    qkv_sends, qkv_sums = swap_out_y(comm, qkv, srcs[0], qkv_landed)
+    out_sends, out_sums = swap_out_y(comm, out, srcs[1], out_landed)
+    exhaust(out_sends, qkv_sends)
+    take_turns(
+        Scatter(comm, p_ref, bufs, total).steps(produce),
+        chain(
+            paired(out_sums, swap_out_z(comm, out, out_landed, dsts[1])),
+            paired(qkv_sums, swap_out_z(comm, qkv, qkv_landed, dsts[0])),
+        ),
+    )
     by_rows(0, rows, back)
     sum_gains(comm, groups, gain_sums, sorted_sums, landed, gain_out)
 
@@ -875,84 +963,74 @@
 
     my_gains = over_groups(norm_gains, 1)
     group_rows = 4 * nz * rows
-    rows_attn, gains, qkv_w, out_w = comm_call(
-        "start", nz, 0, functools.partial(start_work, b),
-        [(block_input, VMEM), (my_gains, VMEM)],
-        [((group_rows, d_model), bf16, ANY), ((2, d_model), f32, VMEM)],
-        [pltpu.VMEM((rows, d_model), bf16), pltpu.VMEM((2, nz) + my_gains.shape, bf16)],
-        [Swap(over_groups(qkv_weight, 1), 1, 2, width, depth, (3, d_model, width)),
-         Swap(over_groups(out_weight, 1), 2, 1, width, depth, (width, d_model))],
-    )
-    qkv_w, out_w = model_order(qkv_w, 1), model_order(out_w, 1)
-
-    score_scale = HD ** (-0.5)
+    n_keys = 2 * b * group_rows
     y, group = lax.axis_index("ctx") % 2, lax.axis_index("ctx") // a
     by_place = positions.reshape(b, nz, 2, n_tp * rows)
     key_pos = by_place.transpose(2, 0, 1, 3).reshape(2 * b, group_rows)
     own_pos = lax.dynamic_index_in_dim(key_pos, y * b + group, 0, keepdims=False)
     cos_tab, sin_tab = rope_tables(own_pos, HD)
-    projected = jnp.einsum("td,kde->kte", rows_attn, qkv_w, preferred_element_type=f32)
-    query_bf = rotate(projected[0], cos_tab, sin_tab, heads, HD).astype(bf16)
-    query_bf = query_bf * jnp.asarray(score_scale, bf16)
-    key_bf = rotate(projected[1], cos_tab, sin_tab, heads, HD).astype(bf16)
-    value_bf = projected[2].astype(bf16)
+    cos_wide = jnp.tile(cos_tab[:, 0, :], (1, 2 * heads))
+    sin_wide = jnp.tile(jnp.concatenate([-sin_tab, sin_tab], axis=-1)[:, 0, :], (1, heads))
     places = [(own_pos[:, None], VMEM), (key_pos.reshape(1, -1), VMEM)]
-    n_keys = 2 * b * group_rows
-    attn_bf, log_total, key_all, value_all, grad_rows, dn_w = comm_call(
-        "attend", nz, 1, functools.partial(attend_work, heads),
-        [(query_bf, VMEM), (over_groups(key_bf, 0), VMEM), (over_groups(value_bf, 0), VMEM)]
-        + places + [(layer_output_gradient, VMEM)],
-        [((group_rows, width), bf16, VMEM), ((group_rows, heads), f32, VMEM),
+    gu_all = over_groups(gate_up_weight, 1)
+    partials = pltpu.VMEM((4 * nz, rows, d_model), bf16)
+    (gains, query_bf, attn_bf, log_total, hidden, rows_attn, key_all, value_all, rows_mlp,
+     qkv_w, out_w, dn_w, gate_w, up_w) = comm_call(
+        "forward", nz, 0, functools.partial(forward_work, heads, b),
+        [(block_input, VMEM), (my_gains, VMEM), (cos_wide, VMEM), (sin_wide, VMEM)] + places,
+        [((2, d_model), f32, VMEM), ((group_rows, width), bf16, VMEM),
+         ((group_rows, width), bf16, VMEM), ((group_rows, heads), f32, VMEM),
+         ((rows, d_model), f32, VMEM), ((group_rows, d_model), bf16, ANY),
          ((n_keys, width), bf16, ANY), ((n_keys, width), bf16, ANY),
          ((group_rows, d_model), bf16, ANY)],
-        [pltpu.VMEM((n_keys, width), bf16), pltpu.VMEM((n_keys, width), bf16)],
-        [Swap(over_groups(down_weight, 1), 2, 1, units, depth, (units, d_model))],
-    )
-    dn_w = model_order(dn_w, 1)
-    gu_all = over_groups(gate_up_weight, 1)
-    partials = pltpu.VMEM((4 * nz, rows, d_model), bf16)
-    hidden, rows_mlp, gate_w, up_w = comm_call(
-        "middle", nz, 2, middle_work,
-        [(attn_bf, VMEM), (out_w, VMEM), (block_input, VMEM), (gains, VMEM)],
-        [((rows, d_model), f32, VMEM), ((group_rows, d_model), bf16, ANY)],
-        [pltpu.VMEM((rows, d_model), bf16), partials] + scatter_bufs(nz, rows, d_model),
-        [Swap(gu_all, 1, 2, units, depth, (d_model, units), p) for p in (0, 1)],
-    )
-    gate_w, up_w = model_order(gate_w, 0), model_order(up_w, 0)
+        [pltpu.VMEM((rows, d_model), bf16), pltpu.VMEM((2, nz) + my_gains.shape, bf16),
+         pltpu.VMEM((group_rows, d_model), bf16), pltpu.VMEM((3, d_model, width), bf16),
+         pltpu.VMEM((width, d_model), bf16), pltpu.VMEM((n_keys, width), bf16),
+         pltpu.VMEM((n_keys, width), bf16), partials]
+        + scatter_bufs(nz, rows, d_model)
+        + [pltpu.VMEM((rows, d_model), bf16), pltpu.VMEM((rows, d_model), f32)],
+        [Swap(over_groups(qkv_weight, 1), 1, 2, width, depth, (3, d_model, width), None, b),
+         Swap(over_groups(out_weight, 1), 2, 1, width, depth, (width, d_model)),
+         Swap(over_groups(down_weight, 1), 2, 1, units, depth, (units, d_model))]
+        + [Swap(gu_all, 1, 2, units, depth, (d_model, units), p, b) for p in (0, 1)],
+        groups=b,
+    )
+    out_w, dn_w = model_order(out_w, 1), model_order(dn_w, 1)
     down_swap = Swap(None, 2, 1, units, depth, (nz * units, depth))
-    residual_grad, branch_rows, gain_sum_2, mlp_part, gu_grad, dn_back = comm_call(
+    half_swap = Swap(None, 1, 2, units, depth, (depth, nz * units))
+    residual_grad, branch_rows, gain_sum_2, block_output, gate_sum, up_grad, dn_back = comm_call(
         "back", nz, 3, functools.partial(back_work, b),
-        [(rows_mlp, ANY), (grad_rows, ANY), (gate_w, VMEM), (up_w, VMEM), (dn_w, VMEM),
+        [(rows_mlp, ANY), (gate_w, VMEM), (up_w, VMEM), (dn_w, VMEM),
          (hidden, VMEM), (layer_output_gradient, VMEM), (gains, VMEM)],
         [((rows, d_model), f32, VMEM), ((group_rows, d_model), bf16, ANY),
-         ((1, d_model), f32, VMEM), ((4 * nz, rows, d_model), bf16, ANY),
-         ((2, d_model, units), bf16, ANY)],
+         ((1, d_model), f32, VMEM), ((rows, d_model), bf16, VMEM),
+         ((nz, depth, units), bf16, ANY), ((d_model, units), bf16, ANY)],
         [pltpu.VMEM((rows, d_model), f32), pltpu.VMEM((rows, d_model), bf16), partials, partials,
-         pltpu.VMEM((3, group_rows, units), bf16),
+         pltpu.VMEM((2, group_rows, units), f32), pltpu.VMEM((3, group_rows, units), bf16),
          pltpu.VMEM((group_rows, d_model), bf16), pltpu.VMEM((group_rows, d_model), bf16),
-         pltpu.VMEM((2, d_model, units), bf16), pltpu.VMEM((units, d_model), bf16),
-         landing(nz, down_swap, (units, d_model))]
-        + scatter_bufs(nz, rows, d_model),
+         pltpu.VMEM((d_model, units), bf16), pltpu.VMEM((d_model, units), bf16),
+         pltpu.VMEM((units, d_model), bf16),
+         landing(nz, down_swap, (units, d_model)), landing(nz, half_swap, (d_model, units))]
+        + scatter_bufs(nz, rows, d_model) + scatter_bufs(nz, rows, d_model),
         [down_swap],
         vmem=60,
+        extra=[half_swap],
     )
     out_weight_grad = jnp.einsum("te,td->ed", attn_bf, branch_rows, preferred_element_type=f32)
     attn_grad_bf = jnp.einsum("td,ed->te", branch_rows, out_w, preferred_element_type=f32).astype(bf16)
-    gu_swap = Swap(gu_grad, 1, 2, units, depth, (2, depth, nz * units))
-    query_grad, key_terms, value_terms, block_output, gu_back = comm_call(
+    query_grad, key_terms, value_terms, gate_back, up_back = comm_call(
         "attend_back", nz, 4, functools.partial(attend_back_work, heads),
         [(query_bf, VMEM), (key_all, VMEM), (value_all, VMEM)] + places
-        + [(attn_bf, VMEM), (log_total, VMEM), (attn_grad_bf, VMEM), (mlp_part, VMEM),
-           (hidden, VMEM)],
+        + [(attn_bf, VMEM), (log_total, VMEM), (attn_grad_bf, VMEM), (gate_sum, VMEM),
+           (up_grad, VMEM)],
         [((group_rows, width), f32, VMEM), ((width, n_keys // 2), f32, VMEM),
-         ((width, n_keys // 2), f32, VMEM), ((rows, d_model), bf16, VMEM)],
-        [pltpu.VMEM((rows, d_model), f32), pltpu.VMEM((width, n_keys), f32),
-         pltpu.VMEM((width, n_keys), f32), pltpu.VMEM((2, width, n_keys // 2), bf16),
-         pltpu.VMEM((2, width, n_keys // 2), bf16), landing(nz, gu_swap, (2, d_model, units))]
-        + scatter_bufs(nz, rows, d_model),
-        [gu_swap],
-        swap_spec=VMEM,
-    )
+         ((width, n_keys // 2), f32, VMEM)],
+        [pltpu.VMEM((width, n_keys), f32), pltpu.VMEM((width, n_keys), f32),
+         pltpu.VMEM((2, width, n_keys // 2), bf16), pltpu.VMEM((2, width, n_keys // 2), bf16),
+         landing(nz, half_swap, (d_model, units))],
+        [half_swap, half_swap],
+    )
+    gu_back = jnp.stack([gate_back, up_back])
     key_grad, value_grad = key_terms.T, value_terms.T
     if b > 1:
         key_grad = to_groups(key_grad.astype(bf16), 0).astype(f32)

time: 588 us -> 491 us (0.84)
  Pallas kernels: 529 us -> 452 us
  local copies, waits for them, and re-layouts: 25.7 us -> 14.3 us
    pallas_call x6 -> x4, Pallas kernels: 529 us -> 452 us  [comm_call(): pl.pallas_call(functools.partial(comm_kernel, nz, groups, work, swaps, li...]
    unnamed x70 -> x52, local copies, waits for them, and re-layouts: 13.4 us -> 8.69 us
where the time goes in v2:
time: 491 us; the launch traced here: 488 us
  Pallas kernels  452 us (92%)
  local copies, waits for them, and re-layouts  14.3 us (3%)
  matrix products  10.3 us (2%)
  other arithmetic  9.96 us (2%)
    pallas_call x4, Pallas kernels, comm_call(): pl.pallas_call(functools.partial(comm_kernel, nz, groups, work, swaps, li...  452 us

profile of v2, /device:TPU:0, one launch (start us, length us, event | category | flops | bytes accessed | tf_op | source)
XLA Modules:
  0.0 488.0 jit_solution(16811101397071865522)
XLA Ops:
  1.4 1.2 fusion.13
  4.4 191.2 %forward.1 = (f32[2,2048]{1,0:T(2,128)S(1)}, bf16[1024,128]{1,0:T(8,128)(2,1)S(1)}, bf16[1024,128]{1,0:T(8,128)(2,1)S(1)}, f32[1024,2]{1,0:T(8,128)S(1)}, f32[64...) custom-call(bf16[64,2048]{1,0:T(8,128)(2,1)S(1)} %copy-done.1, ...), custom_call_target="tpu_custom_call" | custom-call | tf_op jit(solution)/shard_map/forward/pallas_call | solution.py:497
  195.6 0.8 copy-done.4
  196.4 0.8 copy-done.6
  197.2 0.8 copy-done.8
  198.0 0.8 copy-done.18
  199.4 142.4 %back.1 = (f32[64,2048]{1,0:T(8,128)}, bf16[1024,2048]{1,0:T(8,128)(2,1)}, f32[1,2048]{1,0:T(1,128)}, bf16[64,2048]{1,0:T(8,128)(2,1)}, bf16[4,256,512]{2,1,0:T(...) custom-call(bf16[1024,2048]{1,0:T(8,128)(2,1)} %get-tuple-element.37.refs_0_, ...), custom_call_target="tpu_custom_call" | custom-call | tf_op jit(solution)/shard_map/back/pallas_call | solution.py:497
  341.8 3.6 convolution_convert_fusion.1.refs_7_
  346.7 52.9 %attend_back.1 = (f32[1024,128]{1,0:T(8,128)S(1)}, f32[128,1024]{1,0:T(8,128)S(1)}, f32[128,1024]{1,0:T(8,128)S(1)}, bf16[256,2048]{1,0:T(8,128)(2,1)S(1)}, bf16[256,2048]{1,0:T(8,128)(2,1)}) custom-call(bf16[1024,128]{1,0:T(8,128)(2,1)S(1)} %get-tuple-element.44.refs_0_, bf16[2048,128]{1,0:T(8,128)(2,1)S(1)} %copy-done.5, bf16[2048,128]{1,0:T(8,128)(2,1)S(1)} %copy-done.7, ...), custom_call_target="tpu_custom_call" | custom-call | tf_op jit(solution)/shard_map/attend_back/pallas_call | solution.py:497
  399.6 0.8 copy-done.9
  400.4 0.8 copy-done.10
  401.2 0.8 copy-done.12
  402.0 1.3 copy.25
  403.3 1.2 multiply_subtract_fusion.1
  404.9 0.8 copy.30
  405.7 0.8 copy.27
  406.6 1.1 pad_maximum_fusion.refs_0_
  407.8 5.9 %fusion.5.refs_6_ = bf16[3,2048,128]{2,1,0:T(8,128)(2,1)} fusion(bf16[1024,2048]{1,0:T(8,128)(2,1)} %get-tuple-element.59, bf16[1,1024,128]{2,1,0:T(8,128)(2,1)S(1)} %bitcast.52, bf16[1,1024,128]{2,1,0:T(8,128)(2,1)} %copy.30, bf16[1,1024,128]{2,1,0:T(8,128)(2,1)S(1)} %copy.29), kind=kOutput, calls=%fused_computation.3 | convolution fusion | flops 1612185600 | bytes 6553600 | tf_op jit(solution)/shard_map/td,kte->kde/dot_general | solution.py:1042
  413.8 65.8 %last.1 = (f32[64,2048]{1,0:T(8,128)S(1)}, f32[2,256]{1,0:T(2,128)S(1)}, bf16[3,256,512]{2,1,0:T(8,128)(2,1)S(1)}, bf16[512,256]{1,0:T(8,128)(2,1)S(1)}) custom-call(bf16[1024,384]{1,0:T(8,128)(2,1)S(1)} %pad_maximum_fusion.refs_0_, bf16[3,2048,128]{2,1,0:T(8,128)(2,1)S(1)} %copy-done, f32[64,2048]{1,0:T(8,128)S(1)} %copy-done.3, ...), custom_call_target="tpu_custom_call" | custom-call | tf_op jit(solution)/shard_map/last/pallas_call | solution.py:497
  480.3 0.8 convert_element_type.86
  481.1 1.3 convert_element_type.85
  482.5 1.5 convert_element_type.88
  484.0 2.3 maximum_convert_fusion
  487.0 0.8 copy.38
  (62 shorter events, 6.3 us)
Async XLA Ops:
  3.2 1.0 copy-start.1
  3.2 1.2 copy-start.2
  3.2 1.2 copy-start.13
  3.2 1.2 copy-start.17
  195.6 0.8 copy-start.4
  196.4 0.8 copy-start.6
  197.2 0.8 copy-start.8
  198.0 0.8 copy-start.18
  199.4 142.4 %copy-start.19 = (bf16[128,2048]{1,0:T(8,128)(2,1)S(1)}, bf16[128,2048]{1,0:T(8,128)(2,1)}, u32[]{:S(2)}) copy-start(bf16[128,2048]{1,0:T(8,128)(2,1)} %copy-done.18) | copy-start | bytes 1572868
  341.8 3.6 copy-start.20
  345.5 1.0 copy-start.5
  345.5 1.2 copy-start.7
  346.7 56.6 %copy-start.23 = (f32[1024,32]{0,1:T(8,128)S(1)}, f32[1024,32]{0,1:T(8,128)}, u32[]{:S(2)}) copy-start(f32[1024,32]{0,1:T(8,128)} %get-tuple-element.75) | copy-start | bytes 393220
  399.6 0.8 copy-start.9
  400.4 0.8 copy-start.10
  401.2 0.8 copy-start.12
  402.0 2.6 copy-start.11
  407.8 6.0 %copy-start = (bf16[3,2048,128]{2,1,0:T(8,128)(2,1)S(1)}, bf16[3,2048,128]{2,1,0:T(8,128)(2,1)}, u32[]{:S(2)}) copy-start(bf16[3,2048,128]{2,1,0:T(8,128)(2,1)} %get-tuple-element.56.refs_1_) | copy-start | bytes 4718596
  407.8 6.0 %copy-start.3 = (f32[64,2048]{1,0:T(8,128)S(1)}, f32[64,2048]{1,0:T(8,128)}, u32[]{:S(2)}) copy-start(f32[64,2048]{1,0:T(8,128)} %get-tuple-element.57.refs_2_) | copy-start | bytes 1572868
  407.8 6.0 %copy-start.15 = (f32[2,2048]{1,0:T(2,128)S(1)}, f32[2,2048]{1,0:T(2,128)}, u32[]{:S(2)}) copy-start(f32[2,2048]{1,0:T(2,128)} %copy-done.14) | copy-start | bytes 49156
  407.8 6.0 %copy-start.16 = (f32[1,2048]{1,0:T(1,128)S(1)}, f32[1,2048]{1,0:T(1,128)}, u32[]{:S(2)}) copy-start(f32[1,2048]{1,0:T(1,128)} %get-tuple-element.58.refs_5_) | copy-start | bytes 24580
  479.6 2.8 copy-start.21
  482.5 1.6 copy-start.22
  484.0 2.3 copy-start.24
  (1 other events, 0.6 us)

commit v3 on v2

--- a/solution.py
+++ b/solution.py
@@ -259,21 +259,26 @@
 
 
 class Scatter:
-    def __init__(self, comm, p_ref, bufs, total):
+    def __init__(self, comm, p_ref, bufs, total, lo, size):
         nz = comm.at.nz
-        self.comm, self.p_ref, self.bufs, self.total = comm, p_ref, bufs, total
+        self.comm, self.p_ref, self.bufs = comm, p_ref, bufs
+        self.range = pl.ds(lo, size)
+        self.total = total.at[self.range, :]
         self.targets = far_first(comm.at)
         self.sem_k, self.sem_x = comm.sems(2 * nz), comm.sems(nz)
         self.sem_z = comm.used
         comm.sems(2 * nz)
 
+    def buf(self, b, j):
+        return self.bufs[b].at[j, self.range, :]
+
     def mine(self, zi, flip, core):
         x = self.comm.at.x
-        return self.p_ref.at[slot_of(zi, 1 - x if flip else x, core)]
+        return self.p_ref.at[slot_of(zi, 1 - x if flip else x, core), self.range, :]
 
     def passing(self, side, d):
         i = (side + 1) // 2 * self.comm.at.nz + d
-        return self.bufs[2].at[i], self.comm.pool.at[self.sem_z + i]
+        return self.buf(2, i), self.comm.pool.at[self.sem_z + i]
 
     def first(self, t):
         comm, nz, k = self.comm, self.comm.at.nz, self.comm.at.k
@@ -281,7 +286,7 @@
         comm.step(
             [],
             [
-                (self.mine(zi, flip, 1 - k), self.bufs[0].at[flip * nz + zi],
+                (self.mine(zi, flip, 1 - k), self.buf(0, flip * nz + zi),
                  self.sem_k[flip * nz + t], comm.to_k)
                 for flip in (1, 0)
             ],
@@ -290,10 +295,10 @@
     def second(self, t):
         comm, nz, k = self.comm, self.comm.at.nz, self.comm.at.k
         zi = self.targets[t][2]
-        b = self.bufs[0].at[nz + zi]
+        b = self.buf(0, nz + zi)
         comm.step(
             [(b, self.sem_k[nz + t])],
-            [(b, self.bufs[1].at[zi], self.sem_x[t], comm.to_x)],
+            [(b, self.buf(1, zi), self.sem_x[t], comm.to_x)],
             None,
             lambda: add_rows(b, [b, self.mine(zi, 1, k)]),
         )
@@ -302,7 +307,7 @@
         comm, at = self.comm, self.comm.at
         z, nz, k = at.z, at.nz, at.k
         d, side, zi = self.targets[t]
-        b, landed = self.bufs[0].at[zi], self.bufs[1].at[zi]
+        b, landed = self.buf(0, zi), self.buf(1, zi)
         terms = [b, self.mine(zi, 0, k), landed]
         comm.arrive(b, self.sem_k[t])
         comm.arrive(landed, self.sem_x[t])
@@ -469,6 +474,16 @@
     yield from second
 
 
+def lagged(first, second, lag):
+    n = 0
+    for _ in first:
+        n += 1
+        if n > lag:
+            next(second, None)
+        yield
+    yield from second
+
+
 def chain(*many):
     for steps in many:
         yield from steps
@@ -517,8 +532,12 @@
     lax.fori_loop(0, size // step, some_rows, 0)
 
 
-def halves(rows):
-    return [(0, rows // 2), (rows // 2, rows // 2)] if rows % 32 == 0 else [(0, rows)]
+def two_parts(rows):
+    return [(0, rows // 2), (rows // 2, rows // 2)]
+
+
+def making_steps(nz):
+    return 3 * nz - 5
 
 
 def feature_pieces(nz, groups, d_model):
@@ -641,6 +660,12 @@
     yield from row_blocks(q_ref.shape[0], k_ref.shape[0], block)
 
 
+def other_halves(u):
+    width = u.shape[1]
+    low = lax.broadcasted_iota(jnp.int32, (1, width), 1) % HD < HD // 2
+    return jnp.where(low, pltpu.roll(u, width - HD // 2, 1), pltpu.roll(u, HD // 2, 1))
+
+
 def forward_work(heads, groups, comm, swap, ins, outs, scratch):
     x_ref, gain_ref, cos, sin, at_q, at_k = ins
     gains, q_ref, o_ref, lse_ref, hidden, rows_attn, k_out, v_out, rows_mlp = outs
@@ -666,8 +691,7 @@
     by_rows(0, rows, norm_1)
     shards = gather_steps(comm, normed, rows_v, 0, rows)
     advance(shards, z_steps(at))
-    take_turns(shards, chain(out[0], qkv[1]))
-    exhaust(down[0])
+    take_turns(shards, chain(out[0], qkv[1], down[0]))
     qkv[2]()
     comm.keep(qkv_v, dsts[0])
     comm.keep(rows_v, rows_attn)
@@ -677,7 +701,6 @@
 
     group = at.first // (2 * nz)
     mine = [half(ref, group, y) for ref in (k_all, v_all)]
-    low = lax.broadcasted_iota(jnp.int32, (1, width), 1) % HD < HD // 2
 
     def project(i, _):
         r = pl.ds(pl.multiple_of(i * tall, tall), tall)
@@ -685,10 +708,7 @@
 
         def turned(p):
             u = jnp.dot(block, qkv_v[p], preferred_element_type=f32)
-            other = jnp.where(
-                low, pltpu.roll(u, width - HD // 2, 1), pltpu.roll(u, HD // 2, 1)
-            )
-            return (u * cos[r, :] + other * sin[r, :]).astype(bf16)
+            return (u * cos[r, :] + other_halves(u) * sin[r, :]).astype(bf16)
 
         q_ref[r, :] = turned(0) * jnp.asarray(HD ** (-0.5), bf16)
         mine[0][r, :] = turned(1)
@@ -701,8 +721,7 @@
         comm.step([], [(ref, ref, sem[i], comm.to_y)])
         for g, f, device in comm.afar:
             comm.step([], [(ref, ref, sem[2 + (2 * g + f) * 2 + i - 2], device)])
-    exhaust(gate[0])
-    exhaust(out[1])
+    exhaust(gate[0], out[1])
     out[2]()
     comm.keep(out_v, dsts[1])
     for i, (ref, dst) in enumerate(((k_all, k_out), (v_all, v_out))):
@@ -712,7 +731,7 @@
             comm.arrive(come, sem[2 + (2 * g + f) * 2 + i - 2])
         comm.keep(ref, dst)
     take_turns(
-        attend(heads, q_ref, k_all, v_all, at_q, at_k, o_ref, lse_ref), chain(down[1], gate[1])
+        attend(heads, q_ref, k_all, v_all, at_q, at_k, o_ref, lse_ref), chain(down[1], up[0], gate[1])
     )
 
     def norm_2(r):
@@ -725,46 +744,22 @@
         product_into(p_ref, rows, zi * 4, [o_ref[r, :]], [out_v], [0])
 
     normed_2, total = bufs[3], bufs[4]
-    steps = Scatter(comm, p_ref, bufs[:3], total).steps(produce)
-    advance(up[0], 1)
-    exhaust(steps)
-    for c, lo, col, r in feature_pieces(nz, groups, d_model) if groups > 1 else [(0, 0, 0, d_model)]:
-        frm = c * (d_model // (2 * nz)) + lo
-        hidden[:, col : col + r] = total[:, frm : frm + r]
-    by_rows(0, rows, norm_2)
-    shards = gather_steps(comm, normed_2, rows_mlp, 0, rows)
-    advance(shards, z_steps(at))
-    take_turns(shards, up[0])
-    exhaust(up[1])
+
+    def part(lo, size, making):
+        yield from Scatter(comm, p_ref, bufs[:3], total, lo, size).steps(making)
+        r = pl.ds(lo, size)
+        for c, piece, col, n in feature_pieces(nz, groups, d_model) if groups > 1 else [(0, 0, 0, d_model)]:
+            frm = c * (d_model // (2 * nz)) + piece
+            hidden[r, col : col + n] = total[r, frm : frm + n]
+        by_rows(lo, size, norm_2)
+        yield
+        yield from gather_steps(comm, normed_2, rows_mlp, lo, size)
+
+    front, rear = [part(lo, size, None if lo else produce) for lo, size in two_parts(rows)]
+    advance(front, making_steps(nz))
+    take_turns(lagged(front, rear, 1), up[1])
     for one in (down, gate, up):
         one[2]()
-
-
-def attend_back_work(heads, comm, swap, ins, outs, scratch):
-    q_ref, k_ref, v_ref, at_q, at_k, o_ref, lse_ref, do_ref, gate_sum, up_grad = ins
-    dq_ref, dk_out, dv_out = outs
-    dk_ref, dv_ref, going, come, up_landed = scratch
-    (gate, up), _, dsts = swap
-    at = comm.at
-    y, keys = at.y, k_ref.shape[0] // 2
-
-    def half(ref, yy):
-        return ref.at[:, pl.ds(pl.multiple_of(yy * keys, keys), keys)]
-
-    sends, sums = swap_out_y(comm, up, up_grad, up_landed)
-    exhaust(sends)
-    exhaust(swap_out_z(comm, gate, gate_sum, dsts[0]))
-    compute = attend_back(
-        heads, q_ref, k_ref, v_ref, at_q, at_k, o_ref, lse_ref, do_ref, dq_ref, dk_ref, dv_ref
-    )
-    take_turns(compute, paired(sums, swap_out_z(comm, up, up_landed, dsts[1])))
-    sem = comm.sems(2)
-    for i, ref in enumerate((dk_ref, dv_ref)):
-        going[i] = half(ref, 1 - y)[...].astype(bf16)
-        comm.step([], [(going.at[i], come.at[i], sem[i], comm.to_y)])
-    for i, (ref, dst) in enumerate(((dk_ref, dk_out), (dv_ref, dv_out))):
-        comm.arrive(come.at[i], sem[i])
-        dst[...] = half(ref, y)[...] + come[i].astype(f32)
 
 
 def norm_back(grad, unit, rms, gain):
@@ -776,7 +771,7 @@
     rows_mlp, gate_w, up_w, dn_w, hidden, dy_ref, gains = ins
     residual, branch_rows, gain_sum, block_out, gate_out, up_out = outs
     total, rounded, p_ref, q_ref, pre, gates, n2, dy, gate_g, up_g, dn_g, dn_landed, gate_landed = scratch[:13]
-    bufs, bufs_q = scratch[13:16], scratch[16:19]
+    bufs, bufs_q, total_q = scratch[13:16], scratch[16:19], scratch[19]
     (down, gate_swap), _, dsts = swap
     at = comm.at
     nz = at.nz
@@ -789,9 +784,8 @@
         r = pl.ds(pl.multiple_of(zi * tall, tall), tall)
         return pltpu.make_async_copy(rows_mlp.at[r, :], n2.at[r, :], sems[t])
 
-    main = Scatter(comm, p_ref, bufs, total)
-    for t in range(nz):
-        load(t, main.targets[t][2]).start()
+    for t, target in enumerate(far_first(at)):
+        load(t, target[2]).start()
     turn = iter(range(nz))
 
     def forward(zi):
@@ -829,7 +823,7 @@
         rounded[r, :] = dh.astype(bf16)
 
     def out(r):
-        block_out[r, :] = (hidden[r, :] + residual[r, :]).astype(bf16)
+        block_out[r, :] = (hidden[r, :] + total_q[r, :]).astype(bf16)
 
     def gradients(which):
         d_model = n2.shape[1]
@@ -850,39 +844,99 @@
                     ).astype(bf16)
             yield
 
+    def output():
+        yield from Scatter(comm, q_ref, bufs_q, total_q, 0, rows).steps(forward)
+        by_rows(0, rows, out)
+
+    def part(lo, size, making):
+        yield from Scatter(comm, p_ref, bufs, total, lo, size).steps(making)
+        by_rows(lo, size, back)
+        yield
+        yield from gather_steps(comm, rounded, branch_rows, lo, size)
+
     shards = gather_steps(comm, dy_ref, dy, 0, rows)
-    side = Scatter(comm, q_ref, bufs_q, residual).steps(forward)
+    side = output()
     advance(shards, 1)
-    for _ in range(3 * nz - 3):
+    for _ in range(making_steps(nz)):
         next(side)
         advance(shards, 1)
-    take_turns(shards, side)
-    by_rows(0, rows, out)
-    steps = main.steps(backward)
+    for _ in shards:
+        next(side, None)
+    front, rear = [part(lo, size, None if lo else backward) for lo, size in two_parts(rows)]
+    for _ in range(making_steps(nz)):
+        next(front)
+        advance(side, 1)
     down_sends, down_sums = swap_out_y(comm, down, dn_g, dn_landed)
     gate_sends, gate_sums = swap_out_y(comm, gate_swap, gate_g, gate_landed)
-    advance(steps, 3 * nz - 3)
-    take_turns(
-        steps,
-        chain(gradients(2), down_sends, gradients(0), gate_sends, gradients(1)),
-    )
-    comm.keep(up_g, up_out)
-    by_rows(0, rows, back)
-    shards = gather_steps(comm, rounded, branch_rows, 0, rows)
-    advance(shards, z_steps(at))
-    take_turns(shards, paired(down_sums, swap_out_z(comm, down, dn_landed, dsts[0])))
-    exhaust(gate_sums)
+
+    def weights():
+        yield from gradients(2)
+        yield from down_sends
+        yield from gradients(0)
+        yield from gate_sends
+        yield from gradients(1)
+        comm.keep(up_g, up_out)
+        yield from paired(down_sums, swap_out_z(comm, down, dn_landed, dsts[0]))
+        yield from gate_sums
+
+    take_turns(lagged(front, rear, 1), side, weights())
     comm.keep(gate_landed, gate_out)
 
 
-def last_work(groups, comm, swap, ins, outs, scratch):
-    proj_grads, qkv_w, residual, x_ref, gains, gain_sum_2 = ins
+def tail_work(heads, groups, comm, swap, ins, outs, scratch):
+    (q_ref, k_ref, v_ref, at_q, at_k, o_ref, lse_ref, do_ref, gate_sum, up_grad, out_grad,
+     rows_attn, cos, sin, qkv_w, residual, x_ref, gains, gain_sum_2) = ins
     grad_in, gain_out = outs
-    total, gain_sums, sorted_sums, landed, qkv_landed, out_landed, p_ref = scratch[:7]
-    bufs = scratch[7:]
-    rows = x_ref.shape[0]
+    (dq_ref, dk_ref, dv_ref, going, come, up_landed, out_landed, qkv_landed, proj, qkv_g,
+     total, gain_sums, sorted_sums, landed, p_ref) = scratch[:15]
+    bufs = scratch[15:]
+    (gate, up, out, qkv), _, dsts = swap
+    at = comm.at
+    y, nz = at.y, at.nz
+    keys, width = q_ref.shape
+    rows, d_model = x_ref.shape
+    tall = 4 * rows
     gain_sums[0:1, :] = jnp.zeros_like(gain_sum_2)
     gain_sums[1:2, :] = gain_sum_2[...]
+
+    up_sends, up_sums = swap_out_y(comm, up, up_grad, up_landed)
+    out_sends, out_sums = swap_out_y(comm, out, out_grad, out_landed)
+    exhaust(up_sends, out_sends, swap_out_z(comm, gate, gate_sum, dsts[0]))
+    more = chain(
+        paired(up_sums, swap_out_z(comm, up, up_landed, dsts[1])),
+        paired(out_sums, swap_out_z(comm, out, out_landed, dsts[2])),
+    )
+    compute = attend_back(
+        heads, q_ref, k_ref, v_ref, at_q, at_k, o_ref, lse_ref, do_ref, dq_ref, dk_ref, dv_ref
+    )
+    take_turns(compute, more)
+
+    group = at.first // (2 * nz)
+
+    def share(ref, g, yy):
+        return ref.at[:, pl.ds(pl.multiple_of((yy * groups + g) * keys, keys), keys)]
+
+    others = [(0, 1, comm.to_y)] + comm.afar
+    sem = comm.sems(2 * len(others))
+    for j, (g, f, device) in enumerate(others):
+        for i, ref in enumerate((dk_ref, dv_ref)):
+            theirs = share(ref, (group + g) % groups, y + f * (1 - 2 * y))
+            going[j, i] = theirs[...].astype(bf16)
+            comm.step([], [(going.at[j, i], come.at[j, i], sem[2 * j + i], device)])
+
+    def unturned(u, r):
+        return (u * cos[r, :] - other_halves(u) * sin[r, :]).astype(bf16)
+
+    every = pl.ds(0, keys)
+    proj[:, 0:width] = unturned(dq_ref[...], every)
+    for i, ref in enumerate((dk_ref, dv_ref)):
+        grad = share(ref, group, y)[...]
+        for j in range(len(others)):
+            comm.arrive(come.at[j, i], sem[2 * j + i])
+            grad = grad + come[j, i].astype(f32)
+        grad = grad.T
+        cols = slice((i + 1) * width, (i + 2) * width)
+        proj[:, cols] = unturned(grad, every) if i == 0 else grad.astype(bf16)
 
     def back(r):
         x = x_ref[r, :].astype(f32)
@@ -891,24 +945,32 @@
         gain_sums[0:1, :] += jnp.sum(grad * unit, axis=0, keepdims=True)
         grad_in[r, :] = residual[r, :] + norm_back(grad, unit, rms, gains[0:1, :])
 
-    width = qkv_w.shape[2]
-
     def produce(zi):
-        r = pl.ds(pl.multiple_of(zi * 4 * rows, 4 * rows), 4 * rows)
-        lhs = [proj_grads[r, p * width : (p + 1) * width] for p in range(3)]
+        r = pl.ds(pl.multiple_of(zi * tall, tall), tall)
+        lhs = [proj[r, p * width : (p + 1) * width] for p in range(3)]
         product_into(p_ref, rows, zi * 4, lhs, [qkv_w.at[p] for p in range(3)], [1] * 3)
 
-    (qkv, out), srcs, dsts = swap
-    qkv_sends, qkv_sums = swap_out_y(comm, qkv, srcs[0], qkv_landed)
-    out_sends, out_sums = swap_out_y(comm, out, srcs[1], out_landed)
-    exhaust(out_sends, qkv_sends)
-    take_turns(
-        Scatter(comm, p_ref, bufs, total).steps(produce),
-        chain(
-            paired(out_sums, swap_out_z(comm, out, out_landed, dsts[1])),
-            paired(qkv_sums, swap_out_z(comm, qkv, qkv_landed, dsts[0])),
-        ),
-    )
+    qkv_sends, qkv_sums = swap_out_y(comm, qkv, qkv_g, qkv_landed)
+
+    def weights():
+        depth = d_model // (2 * nz)
+        pieces = feature_pieces(nz, groups, d_model)
+        per = max(1, len(pieces) // 4)
+        for j in range(0, len(pieces), per):
+            for c, lo, col, n in pieces[j : j + per]:
+                grad = lax.dot_general(
+                    rows_attn[:, col : col + n], proj[...], (((0,), (0,)), ((), ())),
+                    preferred_element_type=f32,
+                ).astype(bf16)
+                for p in range(3):
+                    qkv_g[p, c * depth + lo : c * depth + lo + n, :] = grad[:, p * width : (p + 1) * width]
+            yield
+        yield from qkv_sends
+        yield from paired(qkv_sums, swap_out_z(comm, qkv, qkv_landed, dsts[3]))
+
+    steps = Scatter(comm, p_ref, bufs, total, 0, rows).steps(produce)
+    advance(steps, making_steps(nz))
+    take_turns(weights(), steps)
     by_rows(0, rows, back)
     sum_gains(comm, groups, gain_sums, sorted_sums, landed, gain_out)
 
@@ -1011,56 +1073,40 @@
          pltpu.VMEM((d_model, units), bf16), pltpu.VMEM((d_model, units), bf16),
          pltpu.VMEM((units, d_model), bf16),
          landing(nz, down_swap, (units, d_model)), landing(nz, half_swap, (d_model, units))]
-        + scatter_bufs(nz, rows, d_model) + scatter_bufs(nz, rows, d_model),
+        + scatter_bufs(nz, rows, d_model) + scatter_bufs(nz, rows, d_model)
+        + [pltpu.VMEM((rows, d_model), f32)],
         [down_swap],
         vmem=60,
         extra=[half_swap],
     )
     out_weight_grad = jnp.einsum("te,td->ed", attn_bf, branch_rows, preferred_element_type=f32)
     attn_grad_bf = jnp.einsum("td,ed->te", branch_rows, out_w, preferred_element_type=f32).astype(bf16)
-    query_grad, key_terms, value_terms, gate_back, up_back = comm_call(
-        "attend_back", nz, 4, functools.partial(attend_back_work, heads),
+    out_swap = Swap(None, 2, 1, width, depth, (nz * width, depth))
+    qkv_swap = Swap(None, 1, 2, width, depth, (3, depth, nz * width))
+    others = 2 * b - 1
+    layer_input_gradient, gain_sums, gate_back, up_back, out_back, qkv_back = comm_call(
+        "tail", nz, 4, functools.partial(tail_work, heads, b),
         [(query_bf, VMEM), (key_all, VMEM), (value_all, VMEM)] + places
         + [(attn_bf, VMEM), (log_total, VMEM), (attn_grad_bf, VMEM), (gate_sum, VMEM),
-           (up_grad, VMEM)],
-        [((group_rows, width), f32, VMEM), ((width, n_keys // 2), f32, VMEM),
-         ((width, n_keys // 2), f32, VMEM)],
-        [pltpu.VMEM((width, n_keys), f32), pltpu.VMEM((width, n_keys), f32),
-         pltpu.VMEM((2, width, n_keys // 2), bf16), pltpu.VMEM((2, width, n_keys // 2), bf16),
-         landing(nz, half_swap, (d_model, units))],
-        [half_swap, half_swap],
+           (up_grad, VMEM), (swap_order(out_weight_grad.astype(bf16), 1), VMEM),
+           (rows_attn, VMEM), (cos_wide, VMEM), (sin_wide, VMEM), (qkv_w, VMEM),
+           (residual_grad, VMEM), (block_input, VMEM), (gains, VMEM), (gain_sum_2, VMEM)],
+        [((rows, d_model), f32, VMEM), ((2, depth), f32, VMEM)],
+        [pltpu.VMEM((group_rows, width), f32),
+         pltpu.VMEM((width, n_keys), f32), pltpu.VMEM((width, n_keys), f32),
+         pltpu.VMEM((others, 2, width, group_rows), bf16),
+         pltpu.VMEM((others, 2, width, group_rows), bf16),
+         landing(nz, half_swap, (d_model, units)), landing(nz, out_swap, (width, d_model)),
+         landing(nz, qkv_swap, (3, d_model, width)),
+         pltpu.VMEM((group_rows, 3 * width), bf16), pltpu.VMEM((3, d_model, width), bf16),
+         pltpu.VMEM((rows, d_model), f32), pltpu.VMEM((2, d_model), f32),
+         pltpu.VMEM((2, nz, 2, depth), f32), pltpu.VMEM((2 * nz + 3, 2, depth), f32), partials]
+        + scatter_bufs(nz, rows, d_model),
+        [half_swap, half_swap, out_swap, qkv_swap],
+        vmem=56,
+        groups=b,
     )
     gu_back = jnp.stack([gate_back, up_back])
-    key_grad, value_grad = key_terms.T, value_terms.T
-    if b > 1:
-        key_grad = to_groups(key_grad.astype(bf16), 0).astype(f32)
-        value_grad = to_groups(value_grad.astype(bf16), 0).astype(f32)
-    query_raw = unrotate(query_grad, cos_tab, sin_tab, heads, HD).astype(bf16)
-    key_raw = unrotate(key_grad, cos_tab, sin_tab, heads, HD).astype(bf16)
-    value_raw = value_grad.astype(bf16)
-    proj_grads = jnp.concatenate([query_raw, key_raw, value_raw], axis=1)
-    qkv_grad = jnp.einsum(
-        "td,kte->kde", rows_attn, jnp.stack([query_raw, key_raw, value_raw]),
-        preferred_element_type=f32,
-    )
-    qkv_swap = Swap(
-        swap_order(qkv_grad.astype(bf16), 1), 1, 2, width, depth, (3, depth, nz * width)
-    )
-    out_swap = Swap(
-        swap_order(out_weight_grad.astype(bf16), 1), 2, 1, width, depth, (nz * width, depth)
-    )
-    layer_input_gradient, gain_sums, qkv_back, out_back = comm_call(
-        "last", nz, 5, functools.partial(last_work, b),
-        [(proj_grads, VMEM), (qkv_w, VMEM), (residual_grad, VMEM), (block_input, VMEM),
-         (gains, VMEM), (gain_sum_2, VMEM)],
-        [((rows, d_model), f32, VMEM), ((2, depth), f32, VMEM)],
-        [pltpu.VMEM((rows, d_model), f32), pltpu.VMEM((2, d_model), f32),
-         pltpu.VMEM((2, nz, 2, depth), f32), pltpu.VMEM((2 * nz + 3, 2, depth), f32),
-         landing(nz, qkv_swap, (3, d_model, width)), landing(nz, out_swap, (width, d_model)),
-         partials] + scatter_bufs(nz, rows, d_model),
-        [qkv_swap, out_swap],
-        swap_spec=VMEM,
-    )
     if b > 1:
         gain_sums = lax.psum(gain_sums, "ctx", axis_index_groups=across)
     gain_cols = d_model // (n_ctx * n_tp)

time: 491 us -> 462 us (0.941)
  Pallas kernels: 452 us -> 433 us
  local copies, waits for them, and re-layouts: 14.3 us -> 8.99 us
    pallas_call x4 -> x3, Pallas kernels: 452 us -> 433 us  [comm_call(): pl.pallas_call(functools.partial(comm_kernel, nz, groups, work, swaps, li...]
    dot_general x1 -> x0, matrix products: 5.94 us -> none  [body(): jnp.einsum('td,kte->kde', rows_attn, jnp.stack([query_raw, key_raw, value...]
where the time goes in v3:
time: 462 us; the launch traced here: 458 us
  Pallas kernels  433 us (94%)
  other arithmetic  9.08 us (2%)
  local copies, waits for them, and re-layouts  8.99 us (2%)
  matrix products  5.83 us (1%)
    pallas_call x3, Pallas kernels, comm_call(): pl.pallas_call(functools.partial(comm_kernel, nz, groups, work, swaps, li...  433 us

profile of v3, /device:TPU:0, one launch (start us, length us, event | category | flops | bytes accessed | tf_op | source)
XLA Modules:
  0.0 458.0 jit_solution(6377338945357583858)
XLA Ops:
  0.7 0.8 reshape.149
  1.6 0.5 multiply_cosine_fusion
  2.1 0.5 fusion
  2.7 0.2 copy.17.refs_3_.refs_13_
  2.9 0.2 copy.16.refs_2_.refs_12_
  3.1 0.2 copy.18.refs_4_.refs_3_
  3.4 179.0 %forward.1 = (f32[2,2048]{1,0:T(2,128)S(1)}, bf16[1024,128]{1,0:T(8,128)(2,1)S(1)}, bf16[1024,128]{1,0:T(8,128)(2,1)S(1)}, f32[1024,2]{1,0:T(8,128)S(1)}, f32[64...) custom-call(bf16[64,2048]{1,0:T(8,128)(2,1)S(1)} %copy-done.3, ...), custom_call_target="tpu_custom_call" | custom-call | tf_op jit(solution)/shard_map/forward/pallas_call | solution.py:512
  182.5 0.8 copy-done.6
  183.3 0.8 copy-done.7
  184.0 0.8 copy-done.8
  184.8 0.8 copy-done.9
  185.6 0.7 copy-done.10
  186.3 0.6 copy-done.13
  186.9 140.0 %back.1 = (f32[64,2048]{1,0:T(8,128)}, bf16[1024,2048]{1,0:T(8,128)(2,1)}, f32[1,2048]{1,0:T(1,128)}, bf16[64,2048]{1,0:T(8,128)(2,1)}, bf16[4,256,512]{2,1,0:T(...) custom-call(bf16[1024,2048]{1,0:T(8,128)(2,1)} %get-tuple-element.34.refs_0_, ...), custom_call_target="tpu_custom_call" | custom-call | tf_op jit(solution)/shard_map/back/pallas_call | solution.py:512
  327.0 4.3 convolution_convert_fusion.1.refs_7_
  331.2 1.5 convolution_convert_fusion.refs_10_
  332.8 113.9 %tail.1 = (f32[64,2048]{1,0:T(8,128)}, f32[2,256]{1,0:T(2,128)}, bf16[256,2048]{1,0:T(8,128)(2,1)}, bf16[256,2048]{1,0:T(8,128)(2,1)}, bf16[512,256]{1,0:T(8,128)(2,1)}, /*index=5*/bf16[3,256,512]{2,1,0:T(8,128)(2,1)}) custom-call(bf16[1024,128]{1,0:T(8,128)(2,1)} %copy-done.10, bf16[2048,128]{1,0:T(8,128)(2,1)} %copy-done.7, bf16[2048,128]{1,0:T(8,128)(2,1)} %copy-done.8, ...), custom_call_target="tpu_custom_call" | custom-call | tf_op jit(solution)/shard_map/tail/pallas_call | solution.py:512
  446.8 1.5 constant_dynamic-slice_fusion
  448.2 1.8 convert_element_type.33
  450.0 2.5 convert_element_type.32
  452.5 1.5 convert_element_type.35
  454.0 2.3 maximum_convert_fusion
  456.3 0.7 copy.24
  457.0 0.8 copy.25
  (43 shorter events, 0.2 us)
Async XLA Ops:
  0.6 2.7 copy-start.3
  0.6 2.7 copy-start.14
  0.7 2.7 copy-start.11
  0.7 2.7 copy-start.5
  1.6 180.9 %copy-start.12 = (s32[1,2048]{1,0:T(1,128)}, s32[1,2048]{1,0:T(1,128)S(1)}, u32[]{:S(2)}) copy-start(s32[1,2048]{1,0:T(1,128)S(1)} %reshape_reshape.3.refs_5_.refs_4_) | copy-start | bytes 24580
  2.9 179.6 %copy-start = (f32[1024,128]{1,0:T(8,128)}, f32[1024,128]{1,0:T(8,128)S(1)}, u32[]{:S(2)}) copy-start(f32[1024,128]{1,0:T(8,128)S(1)} %copy.17.refs_3_.refs_13_) | copy-start | bytes 1572868
  3.1 179.3 %copy-start.1 = (f32[1024,128]{1,0:T(8,128)}, f32[1024,128]{1,0:T(8,128)S(1)}, u32[]{:S(2)}) copy-start(f32[1024,128]{1,0:T(8,128)S(1)} %copy.16.refs_2_.refs_12_) | copy-start | bytes 1572868
  3.4 323.5 %copy-start.2 = (s32[1024,1]{1,0:T(8,128)}, s32[1024,1]{1,0:T(8,128)S(1)}, u32[]{:S(2)}) copy-start(s32[1024,1]{1,0:T(8,128)S(1)} %copy.18.refs_4_.refs_3_) | copy-start | bytes 12292
  182.5 0.8 copy-start.6
  183.3 0.8 copy-start.7
  184.0 0.8 copy-start.8
  184.8 0.8 copy-start.9
  185.6 0.7 copy-start.10
  186.3 0.6 copy-start.13
  186.9 144.3 %copy-start.4 = (bf16[1024,128]{1,0:T(8,128)(2,1)}, bf16[1024,128]{1,0:T(8,128)(2,1)S(1)}, u32[]{:S(2)}) copy-start(bf16[1024,128]{1,0:T(8,128)(2,1)S(1)} %get-tuple-element.44.refs_5_) | copy-start | bytes 786436
  326.9 4.3 copy-start.15
  332.8 119.7 %copy-start.16 = (bf16[2048,256]{1,0:T(8,128)(2,1)S(1)}, bf16[2048,256]{1,0:T(8,128)(2,1)}, u32[]{:S(2)}) copy-start(bf16[2048,256]{1,0:T(8,128)(2,1)} %get-tuple-element.59) | copy-start | bytes 3145732
  446.7 7.2 %copy-start.17 = (bf16[256,2048]{1,0:T(8,128)(2,1)S(1)}, bf16[256,2048]{1,0:T(8,128)(2,1)}, u32[]{:S(2)}) copy-start(bf16[256,2048]{1,0:T(8,128)(2,1)} %get-tuple-element.57) | copy-start | bytes 3145732
  446.7 7.2 %copy-start.18 = (bf16[256,2048]{1,0:T(8,128)(2,1)S(1)}, bf16[256,2048]{1,0:T(8,128)(2,1)}, u32[]{:S(2)}) copy-start(bf16[256,2048]{1,0:T(8,128)(2,1)} %get-tuple-element.58) | copy-start | bytes 3145732
  452.5 3.8 copy-start.20
  454.0 3.0 copy-start.19

commit v4 on v3

--- a/solution.py
+++ b/solution.py
@@ -578,6 +578,7 @@
         to = at.device((z + d) % nz, y, x, k)
         comm.step([], [(gain_ref, landed.at[y, z], sem[d], to)])
     landed[y, z] = gain_ref[...]
+    yield
     for d in range(1, nz):
         comm.arrive(landed.at[y, (z + nz - d) % nz], sem[d])
     comm.step([], [(landed.at[y], landed.at[y], sem[0], comm.to_y)])
@@ -601,7 +602,7 @@
 
 
 def row_blocks(rows, keys, do):
-    step = math.gcd(rows, 128)
+    step = math.gcd(rows, 256)
     fine = max(16, min(128, 128 * 2048 // keys))
     for i in range(rows // step):
 
@@ -681,8 +682,10 @@
 
     places = (qkv_v, out_v) + tuple(dsts[2:])
     qkv, out, down, gate, up = [swap_in(comm, *v) for v in zip(swaps, srcs, places)]
-    exhaust(qkv[0])
-    gains_of_group(comm, groups, gain_ref, landed, gains)
+    gaining = gains_of_group(comm, groups, gain_ref, landed, gains)
+    advance(gaining, 1)
+    advance(qkv[0], nz - 1)
+    exhaust(gaining, qkv[0])
 
     def norm_1(r):
         x = x_ref[r, :].astype(f32)
@@ -768,16 +771,19 @@
 
 
 def back_work(groups, comm, swap, ins, outs, scratch):
-    rows_mlp, gate_w, up_w, dn_w, hidden, dy_ref, gains = ins
+    rows_mlp, gate_hbm, up_hbm, dn_hbm, hidden, dy_ref, gains = ins
     residual, branch_rows, gain_sum, block_out, gate_out, up_out = outs
     total, rounded, p_ref, q_ref, pre, gates, n2, dy, gate_g, up_g, dn_g, dn_landed, gate_landed = scratch[:13]
-    bufs, bufs_q, total_q = scratch[13:16], scratch[16:19], scratch[19]
+    bufs, bufs_q, total_q, gate_w, up_w, dn_w = scratch[13:16], scratch[16:19], *scratch[19:]
     (down, gate_swap), _, dsts = swap
     at = comm.at
     nz = at.nz
     rows = hidden.shape[0]
     tall = 4 * rows
     gain_sum[...] = jnp.zeros_like(gain_sum)
+    weights_here = [
+        comm.move(src, dst) for src, dst in ((gate_hbm, gate_w), (up_hbm, up_w), (dn_hbm, dn_w))
+    ]
     sems = comm.sems(nz)
 
     def load(t, zi):
@@ -857,6 +863,8 @@
     shards = gather_steps(comm, dy_ref, dy, 0, rows)
     side = output()
     advance(shards, 1)
+    for here in weights_here:
+        here()
     for _ in range(making_steps(nz)):
         next(side)
         advance(shards, 1)
@@ -884,13 +892,15 @@
 
 
 def tail_work(heads, groups, comm, swap, ins, outs, scratch):
-    (q_ref, k_ref, v_ref, at_q, at_k, o_ref, lse_ref, do_ref, gate_sum, up_grad, out_grad,
+    (q_ref, k_ref, v_ref, at_q, at_k, o_ref, lse_ref, branch_rows, out_w, gate_sum, up_grad,
      rows_attn, cos, sin, qkv_w, residual, x_ref, gains, gain_sum_2) = ins
     grad_in, gain_out = outs
-    (dq_ref, dk_ref, dv_ref, going, come, up_landed, out_landed, qkv_landed, proj, qkv_g,
-     total, gain_sums, sorted_sums, landed, p_ref) = scratch[:15]
-    bufs = scratch[15:]
-    (gate, up, out, qkv), _, dsts = swap
+    (dq_ref, dk_ref, dv_ref, going, come, up_landed, out_landed, q_landed, kv_landed, proj, n1,
+     q_g, kv_g, total, gain_sums, sorted_sums, landed, p_ref, dh, do_ref, out_g) = scratch[:21]
+    bufs = scratch[21:]
+    (gate, up, out, q_swap, kv_swap), _, dsts = swap
+    dh_here = comm.move(branch_rows, dh)
+    n1_here = comm.move(rows_attn, n1)
     at = comm.at
     y, nz = at.y, at.nz
     keys, width = q_ref.shape
@@ -900,8 +910,25 @@
     gain_sums[1:2, :] = gain_sum_2[...]
 
     up_sends, up_sums = swap_out_y(comm, up, up_grad, up_landed)
-    out_sends, out_sums = swap_out_y(comm, out, out_grad, out_landed)
-    exhaust(up_sends, out_sends, swap_out_z(comm, gate, gate_sum, dsts[0]))
+    exhaust(up_sends, swap_out_z(comm, gate, gate_sum, dsts[0]))
+    depth = d_model // (2 * nz)
+    pieces = feature_pieces(nz, groups, d_model)
+    dh_here()
+
+    def attention_grads(i, _):
+        r = pl.ds(pl.multiple_of(i * tall, tall), tall)
+        do_ref[r, :] = lax.dot_general(
+            dh[r, :], out_w[...], (((1,), (1,)), ((), ())), preferred_element_type=f32
+        ).astype(bf16)
+        return 0
+
+    lax.fori_loop(0, nz, attention_grads, 0)
+    for c, lo, col, n in pieces:
+        out_g[:, c * depth + lo : c * depth + lo + n] = lax.dot_general(
+            o_ref[...], dh[:, col : col + n], (((0,), (0,)), ((), ())), preferred_element_type=f32
+        ).astype(bf16)
+    out_sends, out_sums = swap_out_y(comm, out, out_g, out_landed)
+    exhaust(out_sends)
     more = chain(
         paired(up_sums, swap_out_z(comm, up, up_landed, dsts[1])),
         paired(out_sums, swap_out_z(comm, out, out_landed, dsts[2])),
@@ -929,6 +956,18 @@
 
     every = pl.ds(0, keys)
     proj[:, 0:width] = unturned(dq_ref[...], every)
+
+    def product(col, n, cols):
+        return lax.dot_general(
+            n1[:, col : col + n], proj[:, cols], (((0,), (0,)), ((), ())),
+            preferred_element_type=f32,
+        ).astype(bf16)
+
+    n1_here()
+    for c, lo, col, n in pieces:
+        q_g[c * depth + lo : c * depth + lo + n, :] = product(col, n, slice(0, width))
+    q_sends, q_sums = swap_out_y(comm, q_swap, q_g, q_landed)
+    exhaust(q_sends)
     for i, ref in enumerate((dk_ref, dv_ref)):
         grad = share(ref, group, y)[...]
         for j in range(len(others)):
@@ -950,23 +989,19 @@
         lhs = [proj[r, p * width : (p + 1) * width] for p in range(3)]
         product_into(p_ref, rows, zi * 4, lhs, [qkv_w.at[p] for p in range(3)], [1] * 3)
 
-    qkv_sends, qkv_sums = swap_out_y(comm, qkv, qkv_g, qkv_landed)
+    kv_sends, kv_sums = swap_out_y(comm, kv_swap, kv_g, kv_landed)
 
     def weights():
-        depth = d_model // (2 * nz)
-        pieces = feature_pieces(nz, groups, d_model)
         per = max(1, len(pieces) // 4)
         for j in range(0, len(pieces), per):
             for c, lo, col, n in pieces[j : j + per]:
-                grad = lax.dot_general(
-                    rows_attn[:, col : col + n], proj[...], (((0,), (0,)), ((), ())),
-                    preferred_element_type=f32,
-                ).astype(bf16)
-                for p in range(3):
-                    qkv_g[p, c * depth + lo : c * depth + lo + n, :] = grad[:, p * width : (p + 1) * width]
+                grad = product(col, n, slice(width, 3 * width))
+                for p in (0, 1):
+                    kv_g[p, c * depth + lo : c * depth + lo + n, :] = grad[:, p * width : (p + 1) * width]
             yield
-        yield from qkv_sends
-        yield from paired(qkv_sums, swap_out_z(comm, qkv, qkv_landed, dsts[3]))
+        yield from kv_sends
+        yield from paired(q_sums, swap_out_z(comm, q_swap, q_landed, dsts[3]))
+        yield from paired(kv_sums, swap_out_z(comm, kv_swap, kv_landed, dsts[4]))
 
     steps = Scatter(comm, p_ref, bufs, total, 0, rows).steps(produce)
     advance(steps, making_steps(nz))
@@ -1014,13 +1049,6 @@
             return v
         s = v.shape
         w = v.reshape(s[:axis] + (a, b, depth // b) + s[axis + 1 :])
-        return jnp.swapaxes(w, axis, axis + 1).reshape(s)
-
-    def swap_order(v, axis):
-        if b == 1:
-            return v
-        s = v.shape
-        w = v.reshape(s[:axis] + (b, a, depth // b) + s[axis + 1 :])
         return jnp.swapaxes(w, axis, axis + 1).reshape(s)
 
     my_gains = over_groups(norm_gains, 1)
@@ -1062,7 +1090,7 @@
     half_swap = Swap(None, 1, 2, units, depth, (depth, nz * units))
     residual_grad, branch_rows, gain_sum_2, block_output, gate_sum, up_grad, dn_back = comm_call(
         "back", nz, 3, functools.partial(back_work, b),
-        [(rows_mlp, ANY), (gate_w, VMEM), (up_w, VMEM), (dn_w, VMEM),
+        [(rows_mlp, ANY), (gate_w, ANY), (up_w, ANY), (dn_w, ANY),
          (hidden, VMEM), (layer_output_gradient, VMEM), (gains, VMEM)],
         [((rows, d_model), f32, VMEM), ((group_rows, d_model), bf16, ANY),
          ((1, d_model), f32, VMEM), ((rows, d_model), bf16, VMEM),
@@ -1074,22 +1102,22 @@
          pltpu.VMEM((units, d_model), bf16),
          landing(nz, down_swap, (units, d_model)), landing(nz, half_swap, (d_model, units))]
         + scatter_bufs(nz, rows, d_model) + scatter_bufs(nz, rows, d_model)
-        + [pltpu.VMEM((rows, d_model), f32)],
+        + [pltpu.VMEM((rows, d_model), f32), pltpu.VMEM((d_model, units), bf16),
+           pltpu.VMEM((d_model, units), bf16), pltpu.VMEM((units, d_model), bf16)],
         [down_swap],
         vmem=60,
         extra=[half_swap],
     )
-    out_weight_grad = jnp.einsum("te,td->ed", attn_bf, branch_rows, preferred_element_type=f32)
-    attn_grad_bf = jnp.einsum("td,ed->te", branch_rows, out_w, preferred_element_type=f32).astype(bf16)
     out_swap = Swap(None, 2, 1, width, depth, (nz * width, depth))
-    qkv_swap = Swap(None, 1, 2, width, depth, (3, depth, nz * width))
+    q_swap = Swap(None, 1, 2, width, depth, (depth, nz * width))
+    kv_swap = Swap(None, 1, 2, width, depth, (2, depth, nz * width))
     others = 2 * b - 1
-    layer_input_gradient, gain_sums, gate_back, up_back, out_back, qkv_back = comm_call(
+    layer_input_gradient, gain_sums, gate_back, up_back, out_back, q_back, kv_back = comm_call(
         "tail", nz, 4, functools.partial(tail_work, heads, b),
         [(query_bf, VMEM), (key_all, VMEM), (value_all, VMEM)] + places
-        + [(attn_bf, VMEM), (log_total, VMEM), (attn_grad_bf, VMEM), (gate_sum, VMEM),
-           (up_grad, VMEM), (swap_order(out_weight_grad.astype(bf16), 1), VMEM),
-           (rows_attn, VMEM), (cos_wide, VMEM), (sin_wide, VMEM), (qkv_w, VMEM),
+        + [(attn_bf, VMEM), (log_total, VMEM), (branch_rows, ANY), (out_w, VMEM), (gate_sum, VMEM),
+           (up_grad, VMEM),
+           (rows_attn, ANY), (cos_wide, VMEM), (sin_wide, VMEM), (qkv_w, VMEM),
            (residual_grad, VMEM), (block_input, VMEM), (gains, VMEM), (gain_sum_2, VMEM)],
         [((rows, d_model), f32, VMEM), ((2, depth), f32, VMEM)],
         [pltpu.VMEM((group_rows, width), f32),
@@ -1097,16 +1125,20 @@
          pltpu.VMEM((others, 2, width, group_rows), bf16),
          pltpu.VMEM((others, 2, width, group_rows), bf16),
          landing(nz, half_swap, (d_model, units)), landing(nz, out_swap, (width, d_model)),
-         landing(nz, qkv_swap, (3, d_model, width)),
-         pltpu.VMEM((group_rows, 3 * width), bf16), pltpu.VMEM((3, d_model, width), bf16),
+         landing(nz, q_swap, (d_model, width)), landing(nz, kv_swap, (2, d_model, width)),
+         pltpu.VMEM((group_rows, 3 * width), bf16), pltpu.VMEM((group_rows, d_model), bf16),
+         pltpu.VMEM((d_model, width), bf16), pltpu.VMEM((2, d_model, width), bf16),
          pltpu.VMEM((rows, d_model), f32), pltpu.VMEM((2, d_model), f32),
-         pltpu.VMEM((2, nz, 2, depth), f32), pltpu.VMEM((2 * nz + 3, 2, depth), f32), partials]
+         pltpu.VMEM((2, nz, 2, depth), f32), pltpu.VMEM((2 * nz + 3, 2, depth), f32), partials,
+         pltpu.VMEM((group_rows, d_model), bf16), pltpu.VMEM((group_rows, width), bf16),
+         pltpu.VMEM((width, d_model), bf16)]
         + scatter_bufs(nz, rows, d_model),
-        [half_swap, half_swap, out_swap, qkv_swap],
-        vmem=56,
+        [half_swap, half_swap, out_swap, q_swap, kv_swap],
+        vmem=63,
         groups=b,
     )
     gu_back = jnp.stack([gate_back, up_back])
+    qkv_back = jnp.concatenate([q_back[None], kv_back])
     if b > 1:
         gain_sums = lax.psum(gain_sums, "ctx", axis_index_groups=across)
     gain_cols = d_model // (n_ctx * n_tp)

time: 462 us -> 457 us (0.989)
  matrix products: 5.83 us -> 0 us
  Pallas kernels: 433 us -> 428 us
    dot_general x2 -> x0, matrix products: 5.83 us -> none  [the longest x1 4.28 us: body(): jnp.einsum('td,ed->te', branch_rows, out_w, preferred_element_type=f32)]
    pallas_call x3, Pallas kernels: 433 us -> 428 us  [comm_call(): pl.pallas_call(functools.partial(comm_kernel, nz, groups, work, swaps, li...]
where the time goes in v4:
time: 457 us; the launch traced here: 450 us
  Pallas kernels  428 us (94%)
  local copies, waits for them, and re-layouts  11.7 us (3%)
  other arithmetic  8.94 us (2%)
    pallas_call x3, Pallas kernels, comm_call(): pl.pallas_call(functools.partial(comm_kernel, nz, groups, work, swaps, li...  428 us

profile of v4, /device:TPU:0, one launch (start us, length us, event | category | flops | bytes accessed | tf_op | source)
XLA Modules:
  0.0 450.1 jit_solution(7510597016879440406)
XLA Ops:
  0.7 0.7 reshape.149
  1.4 0.5 multiply_cosine_fusion
  1.9 0.5 fusion
  3.0 0.2 copy.18.refs_4_.refs_3_
  3.4 0.3 copy-done.4
  3.7 0.9 copy-done.12
  4.7 177.1 %forward.1 = (f32[2,2048]{1,0:T(2,128)S(1)}, bf16[1024,128]{1,0:T(8,128)(2,1)S(1)}, bf16[1024,128]{1,0:T(8,128)(2,1)S(1)}, f32[1024,2]{1,0:T(8,128)S(1)}, f32[64...) custom-call(bf16[64,2048]{1,0:T(8,128)(2,1)S(1)} %copy-done.3, ...), custom_call_target="tpu_custom_call" | custom-call | tf_op jit(solution)/shard_map/forward/pallas_call | solution.py:512
  181.8 0.8 copy-done.5
  182.6 0.8 copy-done.6
  183.4 0.8 copy-done.7
  184.1 0.8 copy-done.9
  184.9 0.7 copy-done.10
  185.6 0.7 copy-done.11
  186.3 0.6 copy-done.14
  186.9 137.7 %back.1 = (f32[64,2048]{1,0:T(8,128)}, bf16[1024,2048]{1,0:T(8,128)(2,1)}, f32[1,2048]{1,0:T(1,128)}, bf16[64,2048]{1,0:T(8,128)(2,1)}, bf16[4,256,512]{2,1,0:T(...) custom-call(bf16[1024,2048]{1,0:T(8,128)(2,1)} %get-tuple-element.35.refs_0_, ...), custom_call_target="tpu_custom_call" | custom-call | tf_op jit(solution)/shard_map/back/pallas_call | solution.py:512
  324.7 113.4 %tail.1 = (f32[64,2048]{1,0:T(8,128)}, f32[2,256]{1,0:T(2,128)}, bf16[256,2048]{1,0:T(8,128)(2,1)}, bf16[256,2048]{1,0:T(8,128)(2,1)}, bf16[512,256]{1,0:T(8,128...) custom-call(bf16[1024,128]{1,0:T(8,128)(2,1)} %copy-done.10, bf16[2048,128]{1,0:T(8,128)(2,1)} %copy-done.6, ...), custom_call_target="tpu_custom_call" | custom-call | tf_op jit(solution)/shard_map/tail/pallas_call | solution.py:512
  438.1 1.3 constant_dynamic-slice_fusion
  439.5 1.8 convert_element_type.25
  441.2 2.4 maximum_convert_fusion.1
  443.6 1.5 convert_element_type.27
  445.2 0.7 copy-done.18
  445.9 2.3 maximum_convert_fusion
  448.2 0.7 copy.24
  448.9 0.8 copy.25
  (41 shorter events, 0.8 us)
Async XLA Ops:
  1.4 1.8 copy-start.13
  2.5 1.0 copy-start.3
  2.5 1.2 copy-start.4
  2.5 1.2 copy-start.15
  2.8 179.0 %copy-start = (f32[1024,128]{1,0:T(8,128)}, f32[1024,128]{1,0:T(8,128)S(1)}, u32[]{:S(2)}) copy-start(f32[1024,128]{1,0:T(8,128)S(1)} %copy.17.refs_3_.refs_13_) | copy-start | bytes 1572868
  3.0 178.7 %copy-start.1 = (f32[1024,128]{1,0:T(8,128)}, f32[1024,128]{1,0:T(8,128)S(1)}, u32[]{:S(2)}) copy-start(f32[1024,128]{1,0:T(8,128)S(1)} %copy.16.refs_2_.refs_12_) | copy-start | bytes 1572868
  3.7 1.0 copy-start.12
  4.7 177.1 %copy-start.2 = (s32[1024,1]{1,0:T(8,128)}, s32[1024,1]{1,0:T(8,128)S(1)}, u32[]{:S(2)}) copy-start(s32[1024,1]{1,0:T(8,128)S(1)} %copy.18.refs_4_.refs_3_) | copy-start | bytes 12292
  181.8 0.8 copy-start.5
  182.6 0.8 copy-start.6
  183.3 0.8 copy-start.7
  184.1 0.8 copy-start.9
  184.9 0.7 copy-start.10
  185.6 0.7 copy-start.11
  186.3 0.6 copy-start.14
  186.9 137.7 %copy-start.8 = (bf16[128,2048]{1,0:T(8,128)(2,1)}, bf16[128,2048]{1,0:T(8,128)(2,1)S(1)}, u32[]{:S(2)}) copy-start(bf16[128,2048]{1,0:T(8,128)(2,1)S(1)} %get-tuple-element.48.refs_8_) | copy-start | bytes 1572868
  438.1 5.5 %copy-start.16 = (bf16[2048,256]{1,0:T(8,128)(2,1)S(1)}, bf16[2048,256]{1,0:T(8,128)(2,1)}, u32[]{:S(2)}) copy-start(bf16[2048,256]{1,0:T(8,128)(2,1)} %get-tuple-element.61) | copy-start | bytes 3145732
  443.6 1.6 copy-start.17
  443.6 2.3 copy-start.18
  445.9 2.3 copy-start.20
  445.9 3.0 copy-start.19

commit v5 on v4

--- a/solution.py
+++ b/solution.py
@@ -734,7 +734,7 @@
             comm.arrive(come, sem[2 + (2 * g + f) * 2 + i - 2])
         comm.keep(ref, dst)
     take_turns(
-        attend(heads, q_ref, k_all, v_all, at_q, at_k, o_ref, lse_ref), chain(down[1], up[0], gate[1])
+        attend(heads, q_ref, k_all, v_all, at_q, at_k, o_ref, lse_ref), chain(up[0], down[1], gate[1])
     )
 
     def norm_2(r):
@@ -1083,6 +1083,7 @@
          Swap(over_groups(out_weight, 1), 2, 1, width, depth, (width, d_model)),
          Swap(over_groups(down_weight, 1), 2, 1, units, depth, (units, d_model))]
         + [Swap(gu_all, 1, 2, units, depth, (d_model, units), p, b) for p in (0, 1)],
+        vmem=63,
         groups=b,
     )
     out_w, dn_w = model_order(out_w, 1), model_order(dn_w, 1)

time: 457 us -> 451 us (0.987)
    unnamed x44 -> x12, local copies, waits for them, and re-layouts: 8.91 us -> 2.32 us
where the time goes in v5:
time: 451 us; the launch traced here: 444 us
  Pallas kernels  425 us (94%)
  other arithmetic  8.94 us (2%)
  local copies, waits for them, and re-layouts  8.12 us (2%)
    pallas_call x3, Pallas kernels, comm_call(): pl.pallas_call(functools.partial(comm_kernel, nz, groups, work, swaps, li...  425 us

profile of v5, /device:TPU:0, one launch (start us, length us, event | category | flops | bytes accessed | tf_op | source)
XLA Modules:
  0.0 443.7 jit_solution(13950485376186385466)
XLA Ops:
  0.7 0.7 reshape.149
  1.4 0.6 reshape_reshape.3.refs_5_.refs_4_
  2.0 0.5 multiply_cosine_fusion
  2.5 0.5 fusion
  3.1 1.0 copy.17.refs_3_.refs_13_
  4.2 1.0 copy.16.refs_2_.refs_12_
  5.2 1.0 copy.18.refs_4_.refs_3_
  6.2 177.0 %forward.1 = (f32[2,2048]{1,0:T(2,128)}, bf16[1024,128]{1,0:T(8,128)(2,1)}, bf16[1024,128]{1,0:T(8,128)(2,1)}, f32[1024,2]{1,0:T(8,128)}, f32[64,2048]{1,0:T(8,1...) custom-call(bf16[64,2048]{1,0:T(8,128)(2,1)} %refs_16_.1, ...), custom_call_target="tpu_custom_call" | custom-call | tf_op jit(solution)/shard_map/forward/pallas_call | solution.py:512
  183.2 138.4 %back.1 = (f32[64,2048]{1,0:T(8,128)}, bf16[1024,2048]{1,0:T(8,128)(2,1)}, f32[1,2048]{1,0:T(1,128)}, bf16[64,2048]{1,0:T(8,128)(2,1)}, bf16[4,256,512]{2,1,0:T(...) custom-call(bf16[1024,2048]{1,0:T(8,128)(2,1)} %get-tuple-element.35.refs_0_, ...), custom_call_target="tpu_custom_call" | custom-call | tf_op jit(solution)/shard_map/back/pallas_call | solution.py:512
  321.6 110.1 %tail.1 = (f32[64,2048]{1,0:T(8,128)}, f32[2,256]{1,0:T(2,128)}, bf16[256,2048]{1,0:T(8,128)(2,1)}, bf16[256,2048]{1,0:T(8,128)(2,1)}, bf16[512,256]{1,0:T(8,128...) custom-call(bf16[1024,128]{1,0:T(8,128)(2,1)} %get-tuple-element.42.refs_0_, ...), custom_call_target="tpu_custom_call" | custom-call | tf_op jit(solution)/shard_map/tail/pallas_call | solution.py:512
  431.7 0.0 copy-start
  431.7 1.4 constant_dynamic-slice_fusion
  433.1 1.8 convert_element_type.25
  434.9 2.4 maximum_convert_fusion.1
  437.2 0.0 copy-done
  437.2 0.0 copy-start.1
  437.2 1.5 convert_element_type.27
  438.7 0.1 copy-done.1
  438.8 0.7 copy-done.2
  439.5 2.3 maximum_convert_fusion
  441.8 0.0 copy-done.4
  441.8 0.7 copy.24
  442.5 0.0 copy-done.3
  442.5 0.8 copy.25
  (9 shorter events, 0.1 us)
Async XLA Ops:
  431.7 5.5 %copy-start = (bf16[2048,256]{1,0:T(8,128)(2,1)S(1)}, bf16[2048,256]{1,0:T(8,128)(2,1)}, u32[]{:S(2)}) copy-start(bf16[2048,256]{1,0:T(8,128)(2,1)} %get-tuple-element.61) | copy-start | bytes 3145732
  437.2 1.6 copy-start.1
  437.2 2.3 copy-start.2
  439.5 2.3 copy-start.4
  439.5 3.0 copy-start.3
